TPU v7x, 128 devices: a whole 4x4x4 slice. The times are simulated.
128 devices in a mesh: dp: 64 (over z, y, x), fsdp: 2 (over core).
Axes of the slice: x: 4, y: 4, z: 4, core: 2. Of those that a mesh axis runs over, the one named last changes fastest.
Arguments:
- patches: bfloat16 [4096, 32, 1024], P(('dp', 'fsdp')), may hold values from -6 to 6
- rows: int32 [4096, 32], P(('dp', 'fsdp')), may hold values from 0 to 63
- cols: int32 [4096, 32], P(('dp', 'fsdp')), may hold values from 0 to 63
- keep: int32 [4096, 32], P(('dp', 'fsdp')), may hold values from 0 to 1, as said below
- images: int32 [4096, 32], P(('dp', 'fsdp')), may hold values from 0 to 3, never falling along the last dimension, each value on 1 to 16 neighbouring positions
- destination: int32 [2, 64, 32], P('fsdp'), may hold values from 0 to 63, as said below
- row_table: bfloat16 [64, 1024], replicated, may hold values from -6 to 6
- col_table: bfloat16 [64, 1024], replicated, may hold values from -6 to 6
- w_qkv: bfloat16 [1024, 3072], P('fsdp'), may hold values from -1 to 1
- w_out: bfloat16 [1024, 1024], P('fsdp'), may hold values from -0.1875 to 0.1875
- w_up: bfloat16 [1024, 4096], P('fsdp'), may hold values from -0.1875 to 0.1875
- w_down: bfloat16 [4096, 1024], P('fsdp'), may hold values from -0.09375 to 0.09375
Outputs:
- encoded: bfloat16 [4096, 32, 1024], P(('dp', 'fsdp'))
Inputs may be any that keep to these rules, and one draw needn't show every extreme that they name: keep is 0 or 1; the share of kept tokens differs from sequence to sequence. `destination`: for each fsdp index, every dp index is named by exactly 32 entries of the table, and no row names one dp index more than 1 times.
All inputs are finite; a program needn't handle non-finite values.
Results may differ from a plain program's by a relative error of at most 0.0065.
Values may be sent and summed in bfloat16 or wider, within the bound.
No kernel may reach another device: no remote copies, remote signals or barrier semaphores. Data moves between devices by JAX's collectives and lax.ppermute only.
A program may use at most 192 MiB of HBM per device.

v0:
```python
import jax
import jax.numpy as jnp
from jax import lax
from jax.experimental import pallas as pl
from jax.experimental.pallas import tpu as pltpu
from jax.sharding import PartitionSpec as P


HEADS = 16
HEAD_DIM = 64
BLK = 32
SEQ = 32
D = 1024
MLP = 4096
PEERS = 64
GRID = 64
ROWS = BLK * SEQ
COLS = D // 128
SLOT = COLS * SEQ + 8
GROUP = 4
EPS = 1e-06
MASKED = -1e30
VMEM_LIMIT = 60 * 1024 * 1024
ANY = pl.BlockSpec(memory_space=pl.ANY)
HBM = pl.BlockSpec(memory_space=pltpu.HBM)
SMEM = pl.BlockSpec(memory_space=pltpu.SMEM)
VMEM = pl.BlockSpec(memory_space=pltpu.VMEM)


def norm(values):
    center = values - jnp.mean(values, axis=-1, keepdims=True)
    spread = jnp.mean(center * center, axis=-1, keepdims=True)
    return center * lax.rsqrt(spread + EPS)


def gelu(x):
    inner = x * (0.7978845608028654 + 0.035677408136300125 * (x * x))
    half = 0.5 * x
    return half + half * jnp.tanh(inner)


def embed_body(
    place, table, rows, cols, keep, images, row_table, col_table, patches, out,
    buf, raw, tables, marks, in_sem, sem,
):
    me, side = place[0], place[1]

    def in_copy(g):
        part = pl.ds(g * GROUP, GROUP)
        return pltpu.make_async_copy(patches.at[part], raw.at[part], in_sem.at[g])

    def out_copy(k):
        slot = jnp.where(side == 0, table[0, me, k], k)
        return pltpu.make_async_copy(buf.at[k], out.at[slot], sem.at[k])

    for g in range(BLK // GROUP):
        in_copy(g).start()
    tables[:GRID, :] = row_table[...]
    tables[GRID:, :] = col_table[...]
    label = (keep[...] * (images[...] + 1)).astype(jnp.float32)
    marks[...] = jnp.concatenate([label] * GROUP, axis=1)
    lane = lax.broadcasted_iota(jnp.int32, (SEQ, SEQ), 1)
    line = lax.broadcasted_iota(jnp.int32, (SEQ, SEQ), 0)
    slots = lax.broadcasted_iota(jnp.int32, (SEQ, 2 * GRID), 1).astype(jnp.float32)

    def column(ref, k):
        wide = jnp.broadcast_to(ref[pl.ds(k, 1), :].astype(jnp.float32), (SEQ, SEQ))
        return jnp.sum(jnp.where(lane == line, wide, 0.0), axis=1, keepdims=True)

    def group(g, carry):
        first = g * GROUP
        spots = []
        for j in range(GROUP):
            row, col = column(rows, first + j), column(cols, first + j)
            spots.append(jnp.where((slots == row) | (slots == col + GRID), 1.0, 0.0))
        onehot = jnp.concatenate(spots, axis=0).astype(jnp.bfloat16)
        places = jnp.dot(onehot, tables[...], preferred_element_type=jnp.float32)
        in_copy(g).wait()
        for j in range(GROUP):
            k = first + j
            block = raw[k].astype(jnp.float32) + places[j * SEQ:(j + 1) * SEQ, :]
            block = block.astype(jnp.bfloat16)
            for c in range(COLS):
                buf[k, c * SEQ:(c + 1) * SEQ, :] = block[:, c * 128:(c + 1) * 128]
            mark = jnp.broadcast_to(marks[pl.ds(k, 1), :], (8, 128))
            buf[k, COLS * SEQ:, :] = mark.astype(jnp.bfloat16)
            out_copy(k).start()
        return carry

    lax.fori_loop(0, BLK // GROUP, group, 0)
    for k in range(BLK):
        out_copy(k).wait()


def embed_slots(*operands):
    return pl.pallas_call(
        embed_body,
        out_shape=jax.ShapeDtypeStruct((PEERS, SLOT, 128), jnp.bfloat16),
        in_specs=[SMEM, SMEM] + [VMEM] * 6 + [HBM],
        out_specs=HBM,
        scratch_shapes=[
            pltpu.VMEM((BLK, SLOT, 128), jnp.bfloat16),
            pltpu.VMEM((BLK, SEQ, D), jnp.bfloat16),
            pltpu.VMEM((2 * GRID, D), jnp.bfloat16),
            pltpu.VMEM((BLK, 128), jnp.float32),
            pltpu.SemaphoreType.DMA((BLK // GROUP,)),
            pltpu.SemaphoreType.DMA((BLK,)),
        ],
        compiler_params=pltpu.CompilerParams(vmem_limit_bytes=VMEM_LIMIT),
        name="embed",
    )(*operands)


def sequence(xs, k):
    return jnp.concatenate([xs[k, c * SEQ:(c + 1) * SEQ, :] for c in range(COLS)], axis=1)


def weight_copies(side, own, other, whole, sem, i):
    half = own.shape[0]
    return (
        pltpu.make_async_copy(own, whole.at[pl.ds(side * half, half), :], sem.at[2 * i]),
        pltpu.make_async_copy(
            other, whole.at[pl.ds((1 - side) * half, half), :], sem.at[2 * i + 1]
        ),
    )


def load_sequences(side, order, arrived, sent, xs, sem):
    for k in range(BLK):
        @pl.when(side == 0)
        def _():
            pltpu.make_async_copy(arrived.at[order[k]], xs.at[k], sem.at[k]).start()

        @pl.when(side == 1)
        def _():
            pltpu.make_async_copy(sent.at[k], xs.at[k], sem.at[k]).start()


def await_sequence(sent, xs, sem, k):
    pltpu.make_async_copy(sent.at[k], xs.at[k], sem.at[k]).wait()


def attend_body(
    place, order, arrived, sent, own, other, out,
    xs, w_qkv, normed, qkv, in_sem, w_sem, out_sem,
):
    side = place[1]
    copies = weight_copies(side, own, other, w_qkv, w_sem, 0)

    def out_copy(g):
        part = pl.ds(g * 128, 128)
        return pltpu.make_async_copy(normed.at[part, :], out.at[part, :], out_sem.at[g])

    for copy in copies:
        copy.start()
    load_sequences(side, order, arrived, sent, xs, in_sem)
    for k in range(BLK):
        await_sequence(sent, xs, in_sem, k)

    def first_norm(g, carry):
        for j in range(GROUP):
            k = g * GROUP + j
            x = sequence(xs, k).astype(jnp.float32)
            normed[pl.ds(k * SEQ, SEQ), :] = norm(x).astype(jnp.bfloat16)
        return carry

    lax.fori_loop(0, BLK // GROUP, first_norm, 0)
    for copy in copies:
        copy.wait()

    def project(n, carry):
        for m in range(2):
            part = jnp.dot(
                normed[m * 512:(m + 1) * 512, :], w_qkv[:, pl.ds(n * 512, 512)],
                preferred_element_type=jnp.float32,
            )
            qkv[m * 512:(m + 1) * 512, pl.ds(n * 512, 512)] = part.astype(jnp.bfloat16)
        return carry

    lax.fori_loop(0, 6, project, 0)
    lane = lax.broadcasted_iota(jnp.int32, (128, 128), 1)
    line = lax.broadcasted_iota(jnp.int32, (128, 128), 0)
    low = lane < HEAD_DIM
    zero = jnp.zeros((128, 128), jnp.bfloat16)
    one = jnp.ones((128, 128), jnp.bfloat16)
    ones = jnp.concatenate([jnp.where(low, one, zero), jnp.where(low, zero, one)], axis=0)

    def attend(g, carry):
        base = pl.multiple_of(g * 128, 128)
        label = jnp.zeros((8, 128), jnp.float32)
        for j in range(GROUP):
            marks = xs[g * GROUP + j, COLS * SEQ:, :].astype(jnp.float32)
            label = jnp.where(lane[:8] // SEQ == j, marks, label)
        wide = jnp.broadcast_to(label[:1], (128, 128))
        column = jnp.sum(jnp.where(lane == line, wide, 0.0), axis=1, keepdims=True)
        allowed = (column == wide) & (wide > 0.0) & (lane // SEQ == line // SEQ)
        bias = jnp.where(allowed, 0.0, MASKED)
        bias = jnp.concatenate([bias, bias], axis=0)
        dropped = jnp.where(column == 0.0, 1.0, 0.0)
        for h in range(HEADS // 2):
            q = qkv[pl.ds(base, 128), h * 128:(h + 1) * 128] * jnp.bfloat16(HEAD_DIM ** -0.5)
            key = qkv[pl.ds(base, 128), D + h * 128:D + (h + 1) * 128]
            value = qkv[pl.ds(base, 128), 2 * D + h * 128:2 * D + (h + 1) * 128]
            both = jnp.concatenate([jnp.where(low, q, zero), jnp.where(low, zero, q)], axis=0)
            scores = lax.dot_general(
                both, key, (((1,), (1,)), ((), ())), preferred_element_type=jnp.float32
            )
            scores = scores + bias
            peak = jnp.maximum(jnp.max(scores, axis=1, keepdims=True), 0.1 * MASKED)
            weights = jnp.exp(scores - peak).astype(jnp.bfloat16)
            weights = jnp.concatenate([weights[:128], weights[128:]], axis=1)
            stacked = jnp.concatenate(
                [jnp.where(low, value, zero), jnp.where(low, zero, value)], axis=0
            )
            stacked = jnp.concatenate([stacked, ones], axis=1)
            mixed = jnp.dot(weights, stacked, preferred_element_type=jnp.float32)
            result = mixed[:, :128] / (mixed[:, 128:] + dropped)
            normed[pl.ds(base, 128), h * 128:(h + 1) * 128] = result.astype(jnp.bfloat16)
        out_copy(g).start()
        return carry

    lax.fori_loop(0, BLK // GROUP, attend, 0)
    for g in range(BLK // GROUP):
        out_copy(g).wait()


def attend_kernel(place, order, arrived, sent, own, other):
    bf = jnp.bfloat16
    return pl.pallas_call(
        attend_body,
        out_shape=jax.ShapeDtypeStruct((ROWS, D), bf),
        in_specs=[SMEM, SMEM, HBM, HBM, ANY, ANY],
        out_specs=HBM,
        scratch_shapes=[
            pltpu.VMEM((BLK, SLOT, 128), bf),
            pltpu.VMEM((D, 3 * D), bf),
            pltpu.VMEM((ROWS, D), bf),
            pltpu.VMEM((ROWS, 3 * D), bf),
            pltpu.SemaphoreType.DMA((BLK,)),
            pltpu.SemaphoreType.DMA((2,)),
            pltpu.SemaphoreType.DMA((BLK // GROUP,)),
        ],
        cost_estimate=pl.CostEstimate(
            flops=7_000_000_000, bytes_accessed=12_000_000, transcendentals=2_000_000
        ),
        compiler_params=pltpu.CompilerParams(vmem_limit_bytes=VMEM_LIMIT),
        name="attend",
    )(place, order, arrived, sent, own, other)


def mlp_body(
    place, order, table, attended, arrived, sent, o0, o1, u0, u1, d0, d1, out, results,
    xs, w_out, w_up, w_down, normed, mid, act, outb, live, in_sem, w_sem, out_sem, mix_sem,
):
    me, side = place[0], place[1]
    copies = [
        weight_copies(side, o0, o1, w_out, w_sem, 0),
        weight_copies(side, u0, u1, w_up, w_sem, 1),
        weight_copies(side, d0, d1, w_down, w_sem, 2),
    ]
    mix = pltpu.make_async_copy(attended, normed, mix_sem)
    mix.start()
    for copy in copies[0]:
        copy.start()
    load_sequences(side, order, arrived, sent, xs, in_sem)
    for i in (1, 2):
        for copy in copies[i]:
            copy.start()
    for k in range(BLK):
        await_sequence(sent, xs, in_sem, k)
    lane = lax.broadcasted_iota(jnp.int32, (128, 128), 1)
    line = lax.broadcasted_iota(jnp.int32, (128, 128), 0)

    def alive(g, carry):
        base = pl.multiple_of(g * 128, 128)
        label = jnp.zeros((8, 128), jnp.float32)
        for j in range(GROUP):
            marks = xs[g * GROUP + j, COLS * SEQ:, :].astype(jnp.float32)
            label = jnp.where(lane[:8] // SEQ == j, marks, label)
        wide = jnp.broadcast_to(label[:1], (128, 128))
        column = jnp.sum(jnp.where(lane == line, wide, 0.0), axis=1, keepdims=True)
        live[pl.ds(base, 128), :] = jnp.broadcast_to(column, (128, 128))
        return carry

    lax.fori_loop(0, BLK // GROUP, alive, 0)
    mix.wait()
    for copy in copies[0]:
        copy.wait()

    def merge(m, carry):
        base = pl.multiple_of(m * 256, 256)
        part = jnp.dot(
            normed[pl.ds(base, 256), :], w_out[...], preferred_element_type=jnp.float32
        )
        for j in range(8):
            k = m * 8 + j
            total = sequence(xs, k).astype(jnp.float32) + part[j * SEQ:(j + 1) * SEQ, :]
            mid[pl.ds(k * SEQ, SEQ), :] = total
            normed[pl.ds(k * SEQ, SEQ), :] = norm(total).astype(jnp.bfloat16)
        return carry

    lax.fori_loop(0, 4, merge, 0)
    for copy in copies[1]:
        copy.wait()

    def up(n, carry):
        for m in range(2):
            part = jnp.dot(
                normed[m * 512:(m + 1) * 512, :], w_up[:, pl.ds(n * 512, 512)],
                preferred_element_type=jnp.float32,
            )
            act[m * 512:(m + 1) * 512, pl.ds(n * 512, 512)] = gelu(part).astype(jnp.bfloat16)
        return carry

    lax.fori_loop(0, 8, up, 0)
    for copy in copies[2]:
        copy.wait()

    def down(m, carry):
        base = pl.multiple_of(m * 256, 256)
        part = jnp.dot(act[pl.ds(base, 256), :], w_down[...], preferred_element_type=jnp.float32)
        total = mid[pl.ds(base, 256), :] + part
        total = jnp.where(live[pl.ds(base, 256), :][:, :1] > 0.0, total, 0.0)
        total = total.astype(jnp.bfloat16)
        for j in range(8):
            k = m * 8 + j
            outb[k] = total[j * SEQ:(j + 1) * SEQ, :]

            @pl.when(side == 0)
            def _():
                pltpu.make_async_copy(outb.at[k], out.at[k], out_sem.at[k]).start()

            @pl.when(side == 1)
            def _():
                pltpu.make_async_copy(
                    outb.at[k], results.at[table[0, me, k]], out_sem.at[k]
                ).start()
        return carry

    lax.fori_loop(0, 4, down, 0)
    for k in range(BLK):
        pltpu.make_async_copy(outb.at[k], out.at[k], out_sem.at[k]).wait()


def mlp_kernel(*operands):
    bf, f32 = jnp.bfloat16, jnp.float32
    return pl.pallas_call(
        mlp_body,
        out_shape=(
            jax.ShapeDtypeStruct((BLK, SEQ, D), bf),
            jax.ShapeDtypeStruct((PEERS, SEQ, D), bf),
        ),
        in_specs=[SMEM, SMEM, SMEM] + [HBM] * 9,
        out_specs=(HBM, HBM),
        scratch_shapes=[
            pltpu.VMEM((BLK, SLOT, 128), bf),
            pltpu.VMEM((D, D), bf),
            pltpu.VMEM((D, MLP), bf),
            pltpu.VMEM((MLP, D), bf),
            pltpu.VMEM((ROWS, D), bf),
            pltpu.VMEM((ROWS, D), f32),
            pltpu.VMEM((ROWS, MLP), bf),
            pltpu.VMEM((BLK, SEQ, D), bf),
            pltpu.VMEM((ROWS, 128), f32),
            pltpu.SemaphoreType.DMA((BLK,)),
            pltpu.SemaphoreType.DMA((6,)),
            pltpu.SemaphoreType.DMA((BLK,)),
            pltpu.SemaphoreType.DMA,
        ],
        cost_estimate=pl.CostEstimate(
            flops=20_000_000_000, bytes_accessed=25_000_000, transcendentals=4_000_000
        ),
        compiler_params=pltpu.CompilerParams(vmem_limit_bytes=VMEM_LIMIT),
        name="mlp",
    )(*operands)


def settle_body(place, order, returned, out_in, out, sem):
    @pl.when(place[1] == 1)
    def _():
        for k in range(BLK):
            pltpu.make_async_copy(returned.at[order[k]], out.at[k], sem.at[k]).start()
        for k in range(BLK):
            pltpu.make_async_copy(returned.at[order[k]], out.at[k], sem.at[k]).wait()


def settle_kernel(place, order, returned, out):
    return pl.pallas_call(
        settle_body,
        out_shape=jax.ShapeDtypeStruct(out.shape, out.dtype),
        in_specs=[SMEM, SMEM, HBM, HBM],
        out_specs=HBM,
        scratch_shapes=[pltpu.SemaphoreType.DMA((BLK,))],
        input_output_aliases={3: 0},
        name="settle",
    )(place, order, returned, out)


def blank(like):
    return pl.pallas_call(
        lambda ref, out: None,
        out_shape=jax.ShapeDtypeStruct(like.shape, like.dtype),
        in_specs=[HBM],
        out_specs=HBM,
        name="blank",
    )(like)


def exchange(chosen, values):
    return lax.cond(
        chosen,
        lambda x: lax.all_to_all(x, "dp", split_axis=0, concat_axis=0, tiled=True),
        blank,
        values,
    )


def arrivals(table, myself):
    filled = jnp.any(table == myself, axis=1)
    places = jnp.arange(PEERS, dtype=jnp.int32)
    rank = jnp.sum((filled[None, :] & (places[None, :] < places[:, None])).astype(jnp.int32), axis=1)
    wanted = jnp.arange(BLK, dtype=jnp.int32)
    hit = filled[None, :] & (rank[None, :] == wanted[:, None])
    return jnp.sum(jnp.where(hit, places[None, :], 0), axis=1)


def local(
    patches, rows, cols, keep, images, destination, row_table, col_table, w_qkv, w_out, w_up, w_down
):
    myself = lax.axis_index("dp").astype(jnp.int32)
    side = lax.axis_index("fsdp").astype(jnp.int32)
    place = jnp.stack([myself, side])
    swap = [(0, 1), (1, 0)]
    pairs = []
    for w in (w_qkv, w_out, w_up, w_down):
        pairs.append((w, lax.ppermute(w, "fsdp", swap)))
    sent = embed_slots(
        place, destination, rows, cols, keep, images, row_table, col_table, patches
    )
    order = arrivals(destination[0], myself)
    arrived = exchange(side == 0, sent)
    attended = attend_kernel(place, order, arrived, sent, *pairs[0])
    out, results = mlp_kernel(
        place, order, destination, attended, arrived, sent, *pairs[1], *pairs[2], *pairs[3]
    )
    returned = exchange(side == 1, results)
    return settle_kernel(place, order, returned, out)


def solution(mesh):
    whole = P(("dp", "fsdp"), None, None)
    flat = P(("dp", "fsdp"), None)
    half = P("fsdp", None)
    in_specs = (
        whole, flat, flat, flat, flat, P("fsdp", None, None), P(), P(), half, half, half, half,
    )
    return jax.shard_map(local, mesh=mesh, in_specs=in_specs, out_specs=whole, check_vma=False)
```

profile of v0, /device:TPU:1, one launch (start us, length us, event | category | flops | bytes accessed | tf_op | source)
XLA Modules:
  0.0 182.9 jit_solution(3138575395919392428)
XLA Ops:
  0.0 1.4 collective-permute-start.2
  1.4 0.0 collective-permute-start.3
  1.4 0.5 collective-permute-start
  1.9 0.0 collective-permute-start.1
  1.9 0.6 pad_add_fusion.place
  2.5 1.4 copy.17.table
  3.9 5.7 %embed.1.sent = bf16[64,264,128]{2,1,0:T(8,128)(2,1)} custom-call(s32[2]{0:T(128)} %pad_add_fusion.place, s32[1,64,32]{2,1,0:T(8,128)} %copy.17.table, s32[32,32]{1,0:T(8,128)} %rows.1, s32[32,32]{1,0:T(8,128)} %cols.1, s32[32,32]{1,0:T(8,128)} %keep.1, s32[32,32]{1,0:T(8,128)} %images.1, bf16[64,1024]{1,0:T(8,128)(2,1)} %row_table.1, ...), custom_call_target="tpu_custom_call" | custom-call | tf_op jit(solution)/shard_map/embed/pallas_call | solution.py:96
  9.6 0.0 copy-start
  9.7 0.7 copy-done
  10.4 0.1 convert_reduce_fusion
  10.5 0.7 select_reduce_fusion.order
  11.2 7.7 %collective-permute-done.other = bf16[512,3072]{1,0:T(8,128)(2,1)S(1)} collective-permute-done((bf16[512,3072]{1,0:T(8,128)(2,1)}, bf16[512,3072]{1,0:T(8,128)(2,1)S(1)}, u32[]{:S(2)}, u32[]{:S(2)}) %collective-permute-start) | collective-permute-done | bytes 3145760 | tf_op jit(solution)/shard_map/ppermute | solution.py:436
  18.9 0.0 copy-start.1
  18.9 1.7 copy-done.1
  20.5 19.2 %attend.1.attended = bf16[1024,1024]{1,0:T(8,128)(2,1)} custom-call(s32[2]{0:T(128)} %pad_add_fusion.place, s32[32]{0:T(128)} %select_reduce_fusion.order, bf16[64,264,128]{2,1,0:T(8,128)(2,1)} %get-tuple-element.19.arrived, bf16[64,264,128]{2,1,0:T(8,128)(2,1)} %embed.1.sent, bf16[512,3072]{1,0:T(8,128)(2,1)} %own.1, bf16[512,3072]{1,0:T(8,128)(2,1)} %copy-done.1), custom_call_target="tpu_custom_call" | custom-call | flops 7000000000 | bytes 12000000 | tf_op jit(solution)/shard_map/attend/pallas_call | solution.py:229
  39.7 0.0 collective-permute-done.1.o1
  39.7 0.0 collective-permute-done.2.u1
  39.7 0.0 collective-permute-done.3.d1
  39.7 35.9 %mlp.1 = (bf16[32,32,1024]{2,1,0:T(8,128)(2,1)}, bf16[64,32,1024]{2,1,0:T(8,128)(2,1)}) custom-call(s32[2]{0:T(128)} %pad_add_fusion.place, s32[32]{0:T(128)} %select_reduce_fusion.order, s32[1,64,32]{2,1,0:T(8,128)} %copy.17.table, bf16[1024,1024]{1,0:T(8,128)(2,1)} %attend.1.attended, bf16[64,264,128]{2,1,0:T(8,128)(2,1)} %get-tuple-element.19.arrived, ...), custom_call_target="tpu_custom_call" | custom-call | flops 20000000000 | bytes 25000000 | tf_op jit(solution)/shard_map/mlp/pallas_call | solution.py:347
  75.7 41.7 %conditional.3 = (bf16[64,32,1024]{2,1,0:T(8,128)(2,1)}) conditional(s32[]{:T(128)} %convert_element_type.10, bf16[64,32,1024]{2,1,0:T(8,128)(2,1)} %get-tuple-element.17, bf16[64,32,1024]{2,1,0:T(8,128)(2,1)} %get-tuple-element.17), branch_computations={%region_5.6_spmd, %region_6.7_spmd} | conditional | bytes 8388616 | solution.py:410
  75.7 41.6 %all_to_all.9 = bf16[64,32,1024]{2,1,0:T(8,128)(2,1)} all-to-all(bf16[64,32,1024]{2,1,0:T(8,128)(2,1)} %param.3), channel_id=1, replica_groups=mesh['dp'=64,'fsdp'=2] {'dp'}, dimensions={0} | all-to-all | bytes 8388608 | tf_op jit(solution)/shard_map/cond/branch_1_fun/all_to_all | solution.py:412
  117.3 65.6 %settle.1 = bf16[32,32,1024]{2,1,0:T(8,128)(2,1)} custom-call(s32[2]{0:T(128)} %pad_add_fusion.place, s32[32]{0:T(128)} %select_reduce_fusion.order, bf16[64,32,1024]{2,1,0:T(8,128)(2,1)} %get-tuple-element.20.returned, bf16[32,32,1024]{2,1,0:T(8,128)(2,1)} %get-tuple-element.18.out_in), custom_call_target="tpu_custom_call", output_to_operand_aliasing={{}: (3, {})} | custom-call | tf_op jit(solution)/shard_map/settle/pallas_call | solution.py:388
  (3 shorter events, 0.1 us)
Async XLA Ops:
  0.0 39.7 %collective-permute-start.2 = (bf16[512,4096]{1,0:T(8,128)(2,1)}, bf16[512,4096]{1,0:T(8,128)(2,1)}, u32[]{:S(2)}, u32[]{:S(2)}) collective-permute-start(bf16[512,4096]{1,0:T(8,128)(2,1)} %u0.1), channel_id=1, source_target_pairs={{0,1},{1,0},{2,3},{3,2},{4,5},{5,4},{6,7},{7,6},{8,9},{9,8},{10,11... | collective-permute-start | bytes 12582920 | tf_op jit(solution)/shard_map/ppermute | solution.py:436
  1.4 38.4 %collective-permute-start.3 = (bf16[2048,1024]{1,0:T(8,128)(2,1)}, bf16[2048,1024]{1,0:T(8,128)(2,1)}, u32[]{:S(2)}, u32[]{:S(2)}) collective-permute-start(bf16[2048,1024]{1,0:T(8,128)(2,1)} %d0.1), channel_id=1, source_target_pairs={{0,1},{1,0},{2,3},{3,2},{4,5},{5,4},{6,7},{7,6},{8,9},{9,8},{10,11... | collective-permute-start | bytes 12582920 | tf_op jit(solution)/shard_map/ppermute | solution.py:436
  1.4 17.5 %collective-permute-start = (bf16[512,3072]{1,0:T(8,128)(2,1)}, bf16[512,3072]{1,0:T(8,128)(2,1)S(1)}, u32[]{:S(2)}, u32[]{:S(2)}) collective-permute-start(bf16[512,3072]{1,0:T(8,128)(2,1)} %own.1), channel_id=1, source_target_pairs={{0,1},{1,0},{2,3},{3,2},{4,5},{5,4},{6,7},{7,6},{8,9},{9,8},{10,11... | collective-permute-start | bytes 9437192 | tf_op jit(solution)/shard_map/ppermute | solution.py:436
  1.9 37.8 %collective-permute-start.1 = (bf16[512,1024]{1,0:T(8,128)(2,1)}, bf16[512,1024]{1,0:T(8,128)(2,1)}, u32[]{:S(2)}, u32[]{:S(2)}) collective-permute-start(bf16[512,1024]{1,0:T(8,128)(2,1)} %o0.1), channel_id=1, source_target_pairs={{0,1},{1,0},{2,3},{3,2},{4,5},{5,4},{6,7},{7,6},{8,9},{9,8},{10,11... | collective-permute-start | bytes 3145736 | tf_op jit(solution)/shard_map/ppermute | solution.py:436
  9.6 0.7 copy-start
  18.9 1.7 copy-start.1
where the time goes:
time: 183 us
  Pallas kernels  126 us (69%)
  blocking collectives  41.6 us (23%)
  waiting for transfers between devices  7.69 us (4%)
  local copies, waits for them, and re-layouts  3.74 us (2%)
  starting transfers between devices  1.89 us (1%)
    pallas_call x1, Pallas kernels, settle_kernel(): pl.pallas_call(settle_body, out_shape=jax.ShapeDtypeStruct(out.shape, out...  65.6 us
    all_to_all x1, blocking collectives, exchange(): lax.all_to_all(x, 'dp', split_axis=0, concat_axis=0, tiled=True)  41.6 us
    pallas_call x1, Pallas kernels, mlp_kernel(): pl.pallas_call(mlp_body, out_shape=(jax.ShapeDtypeStruct((BLK, SEQ, D), b...  35.9 us
    pallas_call x1, Pallas kernels, attend_kernel(): pl.pallas_call(attend_body, out_shape=jax.ShapeDtypeStruct((ROWS, D), bf)...  19.2 us
    ppermute x4, waiting for transfers between devices, local(): pairs.append((w, lax.ppermute(w, 'fsdp', swap)))  7.69 us
    pallas_call x1, Pallas kernels, embed_slots(): pl.pallas_call(embed_body, out_shape=jax.ShapeDtypeStruct((PEERS, SLOT, 1...  5.72 us
    unnamed x5, local copies, waits for them, and re-layouts  3.74 us
  transfers between devices with their start and end apart: 4, of which 1 were waited for; matrix products, arithmetic and copies ran while one was open for 2% of the time, Pallas kernels for 14%

commit v1 on v0

--- a/solution.py
+++ b/solution.py
@@ -375,13 +375,22 @@
     )(*operands)
 
 
-def settle_body(place, order, returned, out_in, out, sem):
+def settle_body(place, order, returned, out_in, out, buf, in_sem, out_sem):
+    def in_copy(k):
+        return pltpu.make_async_copy(returned.at[order[k]], buf.at[k], in_sem.at[k])
+
+    def out_copy(k):
+        return pltpu.make_async_copy(buf.at[k], out.at[k], out_sem.at[k])
+
     @pl.when(place[1] == 1)
     def _():
         for k in range(BLK):
-            pltpu.make_async_copy(returned.at[order[k]], out.at[k], sem.at[k]).start()
+            in_copy(k).start()
         for k in range(BLK):
-            pltpu.make_async_copy(returned.at[order[k]], out.at[k], sem.at[k]).wait()
+            in_copy(k).wait()
+            out_copy(k).start()
+        for k in range(BLK):
+            out_copy(k).wait()
 
 
 def settle_kernel(place, order, returned, out):
@@ -390,8 +399,13 @@
         out_shape=jax.ShapeDtypeStruct(out.shape, out.dtype),
         in_specs=[SMEM, SMEM, HBM, HBM],
         out_specs=HBM,
-        scratch_shapes=[pltpu.SemaphoreType.DMA((BLK,))],
+        scratch_shapes=[
+            pltpu.VMEM((BLK, SEQ, D), jnp.bfloat16),
+            pltpu.SemaphoreType.DMA((BLK,)),
+            pltpu.SemaphoreType.DMA((BLK,)),
+        ],
         input_output_aliases={3: 0},
+        compiler_params=pltpu.CompilerParams(vmem_limit_bytes=VMEM_LIMIT),
         name="settle",
     )(place, order, returned, out)
 

time: 183 us -> 121 us (0.66)
  Pallas kernels: 126 us -> 64.3 us
    pallas_call x1, Pallas kernels: 65.6 us -> 3.46 us  [settle_kernel(): pl.pallas_call(settle_body, out_shape=jax.ShapeDtypeStruct(out.shape, out...]
  transfers between devices with their start and end apart: 4 -> 4, of which waited for: 1 -> 1; matrix products, arithmetic and copies ran while one was open for 2% -> 2% of each run, Pallas kernels for 14% -> 21%
where the time goes in v1:
time: 121 us
  Pallas kernels  64.3 us (53%)
  blocking collectives  41.6 us (34%)
  waiting for transfers between devices  7.69 us (6%)
  local copies, waits for them, and re-layouts  3.74 us (3%)
  starting transfers between devices  1.89 us (2%)
  other arithmetic  1.45 us (1%)
    all_to_all x1, blocking collectives, exchange(): lax.all_to_all(x, 'dp', split_axis=0, concat_axis=0, tiled=True)  41.6 us
    pallas_call x1, Pallas kernels, mlp_kernel(): pl.pallas_call(mlp_body, out_shape=(jax.ShapeDtypeStruct((BLK, SEQ, D), b...  35.9 us
    pallas_call x1, Pallas kernels, attend_kernel(): pl.pallas_call(attend_body, out_shape=jax.ShapeDtypeStruct((ROWS, D), bf)...  19.2 us
    ppermute x4, waiting for transfers between devices, local(): pairs.append((w, lax.ppermute(w, 'fsdp', swap)))  7.69 us
    pallas_call x1, Pallas kernels, embed_slots(): pl.pallas_call(embed_body, out_shape=jax.ShapeDtypeStruct((PEERS, SLOT, 1...  5.72 us
    unnamed x5, local copies, waits for them, and re-layouts  3.74 us
    pallas_call x1, Pallas kernels, settle_kernel(): pl.pallas_call(settle_body, out_shape=jax.ShapeDtypeStruct(out.shape, out...  3.46 us
  transfers between devices with their start and end apart: 4, of which 1 were waited for; matrix products, arithmetic and copies ran while one was open for 2% of the time, Pallas kernels for 21%

profile of v1, /device:TPU:1, one launch (start us, length us, event | category | flops | bytes accessed | tf_op | source)
XLA Modules:
  0.0 120.8 jit_solution(12346246014863426730)
XLA Ops:
  0.0 1.4 %collective-permute-start.2 = (bf16[512,4096]{1,0:T(8,128)(2,1)}, bf16[512,4096]{1,0:T(8,128)(2,1)}, u32[]{:S(2)}, u32[]{:S(2)}) collective-permute-start(bf16[512,4096]{1,0:T(8,128)(2,1)} %u0.1), channel_id=1, source_target_pairs={{0,1},{1,0},{2,3},{3,2},{4,5},{5,4},{6,7},{7,6},{8,9},{9,8},{10,11... | collective-permute-start | bytes 12582920 | tf_op jit(solution)/shard_map/ppermute | solution.py:450
  1.4 0.0 collective-permute-start.3
  1.4 0.5 collective-permute-start
  1.9 0.0 collective-permute-start.1
  1.9 0.6 pad_add_fusion.place
  2.5 1.4 %copy.17.table = s32[1,64,32]{2,1,0:T(8,128)} copy(s32[1,64,32]{1,2,0:T(8,128)} %param.21) | data formatting | bytes 16384 | tf_op args[5]
  3.9 5.7 %embed.1.sent = bf16[64,264,128]{2,1,0:T(8,128)(2,1)} custom-call(s32[2]{0:T(128)} %pad_add_fusion.place, s32[1,64,32]{2,1,0:T(8,128)} %copy.17.table, s32[32,32]{1,0:T(8,128)} %rows.1, s32[32,32]{1,0:T(8,128)} %cols.1, s32[32,32]{1,0:T(8,128)} %keep.1, s32[32,32]{1,0:T(8,128)} %images.1, bf16[64,1024]{1,0:T(8,128)(2,1)} %row_table.1, ...), custom_call_target="tpu_custom_call" | custom-call | tf_op jit(solution)/shard_map/embed/pallas_call | solution.py:96
  9.6 0.0 copy-start
  9.7 0.7 copy-done
  10.4 0.1 convert_reduce_fusion
  10.5 0.7 select_reduce_fusion.order
  11.2 7.7 %collective-permute-done.other = bf16[512,3072]{1,0:T(8,128)(2,1)S(1)} collective-permute-done((bf16[512,3072]{1,0:T(8,128)(2,1)}, bf16[512,3072]{1,0:T(8,128)(2,1)S(1)}, u32[]{:S(2)}, u32[]{:S(2)}) %collective-permute-start) | collective-permute-done | bytes 3145760 | tf_op jit(solution)/shard_map/ppermute | solution.py:450
  18.9 0.0 copy-start.1
  18.9 1.7 %copy-done.1 = bf16[512,3072]{1,0:T(8,128)(2,1)} copy-done((bf16[512,3072]{1,0:T(8,128)(2,1)}, bf16[512,3072]{1,0:T(8,128)(2,1)S(1)}, u32[]{:S(2)}) %copy-start.1) | copy-done | bytes 3145752
  20.5 19.2 %attend.1.attended = bf16[1024,1024]{1,0:T(8,128)(2,1)} custom-call(s32[2]{0:T(128)} %pad_add_fusion.place, s32[32]{0:T(128)} %select_reduce_fusion.order, bf16[64,264,128]{2,1,0:T(8,128)(2,1)} %get-tuple-element.19.arrived, bf16[64,264,128]{2,1,0:T(8,128)(2,1)} %embed.1.sent, bf16[512,3072]{1,0:T(8,128)(2,1)} %own.1, bf16[512,3072]{1,0:T(8,128)(2,1)} %copy-done.1), custom_call_target="tpu_custom_call" | custom-call | flops 7000000000 | bytes 12000000 | tf_op jit(solution)/shard_map/attend/pallas_call | solution.py:229
  39.7 0.0 collective-permute-done.1.o1
  39.7 0.0 collective-permute-done.2.u1
  39.7 0.0 collective-permute-done.3.d1
  39.7 35.9 %mlp.1 = (bf16[32,32,1024]{2,1,0:T(8,128)(2,1)}, bf16[64,32,1024]{2,1,0:T(8,128)(2,1)}) custom-call(s32[2]{0:T(128)} %pad_add_fusion.place, s32[32]{0:T(128)} %select_reduce_fusion.order, s32[1,64,32]{2,1,0:T(8,128)} %copy.17.table, bf16[1024,1024]{1,0:T(8,128)(2,1)} %attend.1.attended, bf16[64,264,128]{2,1,0:T(8,128)(2,1)} %get-tuple-element.19.arrived, ...), custom_call_target="tpu_custom_call" | custom-call | flops 20000000000 | bytes 25000000 | tf_op jit(solution)/shard_map/mlp/pallas_call | solution.py:347
  75.7 41.7 %conditional.3 = (bf16[64,32,1024]{2,1,0:T(8,128)(2,1)}) conditional(s32[]{:T(128)} %convert_element_type.10, bf16[64,32,1024]{2,1,0:T(8,128)(2,1)} %get-tuple-element.17, bf16[64,32,1024]{2,1,0:T(8,128)(2,1)} %get-tuple-element.17), branch_computations={%region_5.6_spmd, %region_6.7_spmd} | conditional | bytes 8388616 | solution.py:424
  75.7 41.6 %all_to_all.9 = bf16[64,32,1024]{2,1,0:T(8,128)(2,1)} all-to-all(bf16[64,32,1024]{2,1,0:T(8,128)(2,1)} %param.3), channel_id=1, replica_groups=mesh['dp'=64,'fsdp'=2] {'dp'}, dimensions={0} | all-to-all | bytes 8388608 | tf_op jit(solution)/shard_map/cond/branch_1_fun/all_to_all | solution.py:426
  117.3 3.5 %settle.1 = bf16[32,32,1024]{2,1,0:T(8,128)(2,1)} custom-call(s32[2]{0:T(128)} %pad_add_fusion.place, s32[32]{0:T(128)} %select_reduce_fusion.order, bf16[64,32,1024]{2,1,0:T(8,128)(2,1)} %get-tuple-element.20.returned, bf16[32,32,1024]{2,1,0:T(8,128)(2,1)} %get-tuple-element.18.out_in), custom_call_target="tpu_custom_call", output_to_operand_aliasing={{}: (3, {})} | custom-call | tf_op jit(solution)/shard_map/settle/pallas_call | solution.py:397
  (3 shorter events, 0.1 us)
Async XLA Ops:
  0.0 39.7 %collective-permute-start.2 = (bf16[512,4096]{1,0:T(8,128)(2,1)}, bf16[512,4096]{1,0:T(8,128)(2,1)}, u32[]{:S(2)}, u32[]{:S(2)}) collective-permute-start(bf16[512,4096]{1,0:T(8,128)(2,1)} %u0.1), channel_id=1, source_target_pairs={{0,1},{1,0},{2,3},{3,2},{4,5},{5,4},{6,7},{7,6},{8,9},{9,8},{10,11... | collective-permute-start | bytes 12582920 | tf_op jit(solution)/shard_map/ppermute | solution.py:450
  1.4 38.4 %collective-permute-start.3 = (bf16[2048,1024]{1,0:T(8,128)(2,1)}, bf16[2048,1024]{1,0:T(8,128)(2,1)}, u32[]{:S(2)}, u32[]{:S(2)}) collective-permute-start(bf16[2048,1024]{1,0:T(8,128)(2,1)} %d0.1), channel_id=1, source_target_pairs={{0,1},{1,0},{2,3},{3,2},{4,5},{5,4},{6,7},{7,6},{8,9},{9,8},{10,11... | collective-permute-start | bytes 12582920 | tf_op jit(solution)/shard_map/ppermute | solution.py:450
  1.4 17.5 %collective-permute-start = (bf16[512,3072]{1,0:T(8,128)(2,1)}, bf16[512,3072]{1,0:T(8,128)(2,1)S(1)}, u32[]{:S(2)}, u32[]{:S(2)}) collective-permute-start(bf16[512,3072]{1,0:T(8,128)(2,1)} %own.1), channel_id=1, source_target_pairs={{0,1},{1,0},{2,3},{3,2},{4,5},{5,4},{6,7},{7,6},{8,9},{9,8},{10,11... | collective-permute-start | bytes 9437192 | tf_op jit(solution)/shard_map/ppermute | solution.py:450
  1.9 37.8 %collective-permute-start.1 = (bf16[512,1024]{1,0:T(8,128)(2,1)}, bf16[512,1024]{1,0:T(8,128)(2,1)}, u32[]{:S(2)}, u32[]{:S(2)}) collective-permute-start(bf16[512,1024]{1,0:T(8,128)(2,1)} %o0.1), channel_id=1, source_target_pairs={{0,1},{1,0},{2,3},{3,2},{4,5},{5,4},{6,7},{7,6},{8,9},{9,8},{10,11... | collective-permute-start | bytes 3145736 | tf_op jit(solution)/shard_map/ppermute | solution.py:450
  9.6 0.7 copy-start
  18.9 1.7 %copy-start.1 = (bf16[512,3072]{1,0:T(8,128)(2,1)}, bf16[512,3072]{1,0:T(8,128)(2,1)S(1)}, u32[]{:S(2)}) copy-start(bf16[512,3072]{1,0:T(8,128)(2,1)S(1)} %collective-permute-done.other) | copy-start | bytes 9437188

commit v2 on v1

v2 whole, which is shorter than its diff:
```python
import jax
import jax.numpy as jnp
from jax import lax
from jax.experimental import pallas as pl
from jax.experimental.pallas import tpu as pltpu
from jax.sharding import PartitionSpec as P


HEADS = 16
HEAD_DIM = 64
BLK = 32
SEQ = 32
D = 1024
MLP = 4096
PEERS = 64
GRID = 64
ROWS = BLK * SEQ
COLS = D // 128
SLOT = COLS * SEQ + 8
GROUP = 4
EPS = 1e-06
UP = 512
DOWN = 256
MASKED = -1e30
VMEM_LIMIT = 60 * 1024 * 1024
ATTEND_LIMIT = 36 * 1024 * 1024
WIDE = 512
ANY = pl.BlockSpec(memory_space=pl.ANY)
HBM = pl.BlockSpec(memory_space=pltpu.HBM)
SMEM = pl.BlockSpec(memory_space=pltpu.SMEM)
VMEM = pl.BlockSpec(memory_space=pltpu.VMEM)


def norm(values):
    center = values - jnp.mean(values, axis=-1, keepdims=True)
    spread = jnp.mean(center * center, axis=-1, keepdims=True)
    return center * lax.rsqrt(spread + EPS)


def gelu(x):
    inner = x * (0.7978845608028654 + 0.035677408136300125 * (x * x))
    half = 0.5 * x
    return half + half * jnp.tanh(inner)


def embed_body(
    table, wide_table, rows, cols, keep, images, row_table, col_table, patches, out, order,
    buf, raw, tables, marks, spots, in_sem, sem,
):
    me, side = lax.axis_index("dp"), lax.axis_index("fsdp")

    def in_copy(g):
        part = pl.ds(g * 2 * GROUP, 2 * GROUP)
        return pltpu.make_async_copy(patches.at[part], raw.at[part], in_sem.at[g])

    def out_copy(k):
        slot = jnp.where(side == 0, table[0, k, me], k)
        return pltpu.make_async_copy(buf.at[k], out.at[slot], sem.at[k])

    for g in range(BLK // GROUP // 2):
        in_copy(g).start()
    tables[:GRID, :] = row_table[...]
    tables[GRID:, :] = col_table[...]
    label = (keep[...] * (images[...] + 1)).astype(jnp.float32)
    marks[...] = jnp.concatenate([label] * GROUP, axis=1)
    for i, ref in enumerate((rows, cols)):
        parts = [ref[pl.ds(j, BLK // GROUP, stride=GROUP), :] for j in range(GROUP)]
        spots[i] = jnp.concatenate(parts, axis=1)
    slots = lax.broadcasted_iota(jnp.int32, (2 * GRID, 128), 0)
    for g in range(BLK // GROUP):
        row, col = spots[0, g:g + 1, :], spots[1, g:g + 1, :] + GRID
        onehot = jnp.where((slots == row) | (slots == col), 1.0, 0.0).astype(jnp.bfloat16)
        places = lax.dot_general(
            onehot, tables[...], (((0,), (0,)), ((), ())), preferred_element_type=jnp.float32
        )
        if g % 2 == 0:
            in_copy(g // 2).wait()
        for j in range(GROUP):
            k = g * GROUP + j
            block = raw[k].astype(jnp.float32) + places[j * SEQ:(j + 1) * SEQ, :]
            block = block.astype(jnp.bfloat16)
            for c in range(COLS):
                buf[k, c * SEQ:(c + 1) * SEQ, :] = block[:, c * 128:(c + 1) * 128]
            mark = jnp.broadcast_to(marks[k:k + 1, :], (8, 128))
            buf[k, COLS * SEQ:, :] = mark.astype(jnp.bfloat16)
            out_copy(k).start()
    hits = jnp.where(wide_table[0] == me, 1.0, 0.0)
    filled = jnp.broadcast_to(jnp.max(hits, axis=0, keepdims=True), (BLK, PEERS))
    before = lax.broadcasted_iota(jnp.int32, (PEERS, PEERS), 0)
    after = lax.broadcasted_iota(jnp.int32, (PEERS, PEERS), 1)
    earlier = jnp.where(before < after, 1.0, 0.0).astype(jnp.bfloat16)
    rank = jnp.dot(filled.astype(jnp.bfloat16), earlier, preferred_element_type=jnp.float32)
    wanted = lax.broadcasted_iota(jnp.int32, (BLK, PEERS), 0).astype(jnp.float32)
    source = lax.broadcasted_iota(jnp.int32, (BLK, PEERS), 1).astype(jnp.float32)
    picked = jnp.where((filled > 0.0) & (rank == wanted), source, 0.0)
    picked = jnp.sum(picked, axis=1, keepdims=True)
    order[...] = jnp.broadcast_to(picked, (BLK, 128)).astype(jnp.int32)
    for k in range(BLK):
        out_copy(k).wait()


def embed_slots(*operands):
    return pl.pallas_call(
        embed_body,
        out_shape=(
            jax.ShapeDtypeStruct((PEERS, SLOT, 128), jnp.bfloat16),
            jax.ShapeDtypeStruct((BLK, 128), jnp.int32),
        ),
        in_specs=[SMEM] + [VMEM] * 7 + [HBM],
        out_specs=(HBM, VMEM),
        scratch_shapes=[
            pltpu.VMEM((BLK, SLOT, 128), jnp.bfloat16),
            pltpu.VMEM((BLK, SEQ, D), jnp.bfloat16),
            pltpu.VMEM((2 * GRID, D), jnp.bfloat16),
            pltpu.VMEM((BLK, 128), jnp.float32),
            pltpu.VMEM((2, BLK // GROUP, 128), jnp.int32),
            pltpu.SemaphoreType.DMA((BLK // GROUP // 2,)),
            pltpu.SemaphoreType.DMA((BLK,)),
        ],
        compiler_params=pltpu.CompilerParams(vmem_limit_bytes=VMEM_LIMIT),
        name="embed",
    )(*operands)


def sequence(xs, k):
    return jnp.concatenate([xs[k, c * SEQ:(c + 1) * SEQ, :] for c in range(COLS)], axis=1)


def weight_copies(side, own, other, whole, sem):
    half = own.shape[0]
    return [
        pltpu.make_async_copy(piece, whole.at[pl.ds(row * half, half), :], sem.at[i])
        for i, (piece, row) in enumerate(((own, side), (other, 1 - side)))
    ]


def run(copies, act):
    for copy in copies:
        getattr(copy, act)()


def marks_of(xs, g):
    lane = lax.broadcasted_iota(jnp.int32, (128, 128), 1)
    line = lax.broadcasted_iota(jnp.int32, (128, 128), 0)
    label = jnp.zeros((8, 128), jnp.float32)
    for j in range(GROUP):
        marks = xs[g * GROUP + j, COLS * SEQ:, :].astype(jnp.float32)
        label = jnp.where(lane[:8] // SEQ == j, marks, label)
    wide = jnp.broadcast_to(label[:1], (128, 128))
    column = jnp.sum(jnp.where(lane == line, wide, 0.0), axis=1, keepdims=True)
    return wide, column


def load_sequences(side, order, arrived, sent, xs, sem, low, high):
    for k in range(low, high):
        @pl.when(side == 0)
        def _():
            pltpu.make_async_copy(arrived.at[order[k, 0]], xs.at[k], sem.at[k]).start()

        @pl.when(side == 1)
        def _():
            pltpu.make_async_copy(sent.at[k], xs.at[k], sem.at[k]).start()


def await_sequence(sent, xs, sem, k):
    pltpu.make_async_copy(sent.at[k], xs.at[k], sem.at[k]).wait()


def attend_body(
    order, arrived, sent, own, other, out,
    xs, w_qkv, normed, qkv, mixed, in_sem, w_sem, out_sem,
):
    side = lax.axis_index("fsdp")
    copies = weight_copies(side, own, other, w_qkv, w_sem.at[0])

    def out_copy(g):
        part = pl.ds(g * 128, 128)
        return pltpu.make_async_copy(mixed.at[part, :], out.at[part, :], out_sem.at[g])

    load_sequences(side, order, arrived, sent, xs, in_sem, 0, 8)
    run(copies, "start")
    load_sequences(side, order, arrived, sent, xs, in_sem, 8, BLK)

    def smooth(m, slot):
        for j in range(8):
            x = sequence(xs, m * 8 + j).astype(jnp.float32)
            normed[slot, j * SEQ:(j + 1) * SEQ, :] = norm(x).astype(jnp.bfloat16)

    def project(m, slot):
        base = m * 256 if isinstance(m, int) else pl.multiple_of(m * 256, 256)
        for n in range(3 * D // WIDE):
            part = jnp.dot(
                normed[slot], w_qkv[:, n * WIDE:(n + 1) * WIDE],
                preferred_element_type=jnp.float32,
            )
            qkv[pl.ds(base, 256), n * WIDE:(n + 1) * WIDE] = part.astype(jnp.bfloat16)

    for j in range(8):
        await_sequence(sent, xs, in_sem, j)
    smooth(0, 0)
    for j in range(8, BLK):
        await_sequence(sent, xs, in_sem, j)
    run(copies, "wait")

    def block(m, carry):
        slot = m % 2
        project(m, slot)
        smooth(m + 1, 1 - slot)
        return carry

    lax.fori_loop(0, 3, block, 0)
    project(3, 1)
    lane = lax.broadcasted_iota(jnp.int32, (128, 128), 1)
    line = lax.broadcasted_iota(jnp.int32, (128, 128), 0)
    low = lane < HEAD_DIM
    zero = jnp.zeros((128, 128), jnp.bfloat16)
    one = jnp.ones((128, 128), jnp.bfloat16)
    ones = jnp.concatenate([jnp.where(low, one, zero), jnp.where(low, zero, one)], axis=0)

    def attend(g, carry):
        base = pl.multiple_of(g * 128, 128)
        wide, column = marks_of(xs, g)
        allowed = (column == wide) & (wide > 0.0) & (lane // SEQ == line // SEQ)
        bias = jnp.where(allowed, 0.0, MASKED)
        bias = jnp.concatenate([bias, bias], axis=0)
        dropped = jnp.where(column == 0.0, 1.0, 0.0)
        for h in range(HEADS // 2):
            q = qkv[pl.ds(base, 128), h * 128:(h + 1) * 128] * jnp.bfloat16(HEAD_DIM ** -0.5)
            key = qkv[pl.ds(base, 128), D + h * 128:D + (h + 1) * 128]
            value = qkv[pl.ds(base, 128), 2 * D + h * 128:2 * D + (h + 1) * 128]
            both = jnp.concatenate([jnp.where(low, q, zero), jnp.where(low, zero, q)], axis=0)
            scores = lax.dot_general(
                both, key, (((1,), (1,)), ((), ())), preferred_element_type=jnp.float32
            )
            scores = scores + bias
            peak = jnp.maximum(jnp.max(scores, axis=1, keepdims=True), 0.1 * MASKED)
            weights = jnp.exp(scores - peak).astype(jnp.bfloat16)
            weights = jnp.concatenate([weights[:128], weights[128:]], axis=1)
            stacked = jnp.concatenate(
                [jnp.where(low, value, zero), jnp.where(low, zero, value)], axis=0
            )
            stacked = jnp.concatenate([stacked, ones], axis=1)
            both = jnp.dot(weights, stacked, preferred_element_type=jnp.float32)
            result = both[:, :128] / (both[:, 128:] + dropped)
            mixed[pl.ds(base, 128), h * 128:(h + 1) * 128] = result.astype(jnp.bfloat16)
        out_copy(g).start()
        return carry

    lax.fori_loop(0, BLK // GROUP, attend, 0)
    for g in range(BLK // GROUP):
        out_copy(g).wait()


def attend_kernel(order, arrived, sent, own, other):
    bf = jnp.bfloat16
    return pl.pallas_call(
        attend_body,
        out_shape=jax.ShapeDtypeStruct((ROWS, D), bf),
        in_specs=[SMEM, HBM, HBM, ANY, ANY],
        out_specs=HBM,
        scratch_shapes=[
            pltpu.VMEM((BLK, SLOT, 128), bf),
            pltpu.VMEM((D, 3 * D), bf),
            pltpu.VMEM((2, 256, D), bf),
            pltpu.VMEM((ROWS, 3 * D), bf),
            pltpu.VMEM((ROWS, D), bf),
            pltpu.SemaphoreType.DMA((BLK,)),
            pltpu.SemaphoreType.DMA((1, 2)),
            pltpu.SemaphoreType.DMA((BLK // GROUP,)),
        ],
        cost_estimate=pl.CostEstimate(
            flops=7_000_000_000, bytes_accessed=12_000_000, transcendentals=2_000_000
        ),
        compiler_params=pltpu.CompilerParams(vmem_limit_bytes=ATTEND_LIMIT),
        name="attend",
    )(order, arrived, sent, own, other)


def mlp_body(
    order, table, attended, arrived, sent, o0, o1, u0, u1, d0, d1, out, results,
    xs, w_out, w_up, w_down, normed, second, mid, act, outb, in_sem, w_sem, out_sem, mix_sem,
):
    me, side = lax.axis_index("dp"), lax.axis_index("fsdp")
    proj = weight_copies(side, o0, o1, w_out, w_sem.at[0])
    ups = weight_copies(side, u0, u1, w_up, w_sem.at[1])
    downs = weight_copies(side, d0, d1, w_down, w_sem.at[2])

    def mix_copy(m):
        part = pl.ds(m * 256, 256)
        return pltpu.make_async_copy(attended.at[part, :], normed.at[part, :], mix_sem.at[m])

    mix_copy(0).start()
    run(proj, "start")
    load_sequences(side, order, arrived, sent, xs, in_sem, 0, 8)
    run(ups + downs, "start")
    load_sequences(side, order, arrived, sent, xs, in_sem, 8, BLK)
    for m in range(1, 4):
        mix_copy(m).start()

    def block(m, first):
        base = m * 256 if first else pl.multiple_of(m * 256, 256)
        mix_copy(m).wait()
        if first:
            run(proj, "wait")
        for j in range(8):
            await_sequence(sent, xs, in_sem, m * 8 + j)
        columns = jnp.concatenate([marks_of(xs, m * 2 + g)[1] for g in range(2)], axis=0)
        part = jnp.dot(
            normed[pl.ds(base, 256), :], w_out[...], preferred_element_type=jnp.float32
        )
        for j in range(8):
            k = m * 8 + j
            total = sequence(xs, k).astype(jnp.float32) + part[j * SEQ:(j + 1) * SEQ, :]
            mid[j * SEQ:(j + 1) * SEQ, :] = total
            second[j * SEQ:(j + 1) * SEQ, :] = norm(total).astype(jnp.bfloat16)
        if first:
            run(ups, "wait")
        for n in range(MLP // UP):
            upper = jnp.dot(
                second[...], w_up[:, n * UP:(n + 1) * UP], preferred_element_type=jnp.float32
            )
            act[:, n * UP:(n + 1) * UP] = gelu(upper).astype(jnp.bfloat16)
        if first:
            run(downs, "wait")
        for n in range(D // DOWN):
            lower = jnp.dot(
                act[...], w_down[:, n * DOWN:(n + 1) * DOWN], preferred_element_type=jnp.float32
            )
            total = mid[:, n * DOWN:(n + 1) * DOWN] + lower
            total = jnp.where(columns > 0.0, total, 0.0).astype(jnp.bfloat16)
            for j in range(8):
                outb[m * 8 + j, :, n * DOWN:(n + 1) * DOWN] = total[j * SEQ:(j + 1) * SEQ, :]
        for j in range(8):
            k = m * 8 + j

            @pl.when(side == 0)
            def _():
                pltpu.make_async_copy(outb.at[k], out.at[k], out_sem.at[k]).start()

            @pl.when(side == 1)
            def _():
                pltpu.make_async_copy(
                    outb.at[k], results.at[table[0, k, me]], out_sem.at[k]
                ).start()

    block(0, True)
    lax.fori_loop(1, 4, lambda m, carry: (block(m, False), carry)[1], 0)
    for k in range(BLK):
        pltpu.make_async_copy(outb.at[k], out.at[k], out_sem.at[k]).wait()


def mlp_kernel(*operands):
    bf, f32 = jnp.bfloat16, jnp.float32
    return pl.pallas_call(
        mlp_body,
        out_shape=(
            jax.ShapeDtypeStruct((BLK, SEQ, D), bf),
            jax.ShapeDtypeStruct((PEERS, SEQ, D), bf),
        ),
        in_specs=[SMEM, SMEM, ANY] + [HBM] * 8,
        out_specs=(HBM, HBM),
        scratch_shapes=[
            pltpu.VMEM((BLK, SLOT, 128), bf),
            pltpu.VMEM((D, D), bf),
            pltpu.VMEM((D, MLP), bf),
            pltpu.VMEM((MLP, D), bf),
            pltpu.VMEM((ROWS, D), bf),
            pltpu.VMEM((256, D), bf),
            pltpu.VMEM((256, D), f32),
            pltpu.VMEM((256, MLP), bf),
            pltpu.VMEM((BLK, SEQ, D), bf),
            pltpu.SemaphoreType.DMA((BLK,)),
            pltpu.SemaphoreType.DMA((3, 2)),
            pltpu.SemaphoreType.DMA((BLK,)),
            pltpu.SemaphoreType.DMA((4,)),
        ],
        cost_estimate=pl.CostEstimate(
            flops=20_000_000_000, bytes_accessed=25_000_000, transcendentals=4_000_000
        ),
        compiler_params=pltpu.CompilerParams(vmem_limit_bytes=VMEM_LIMIT),
        name="mlp",
    )(*operands)


def settle_body(order, returned, out_in, out, buf, in_sem, out_sem):
    def in_copy(k):
        return pltpu.make_async_copy(returned.at[order[k, 0]], buf.at[k], in_sem.at[k])

    def out_copy(k):
        return pltpu.make_async_copy(buf.at[k], out.at[k], out_sem.at[k])

    @pl.when(lax.axis_index("fsdp") == 1)
    def _():
        for k in range(BLK):
            in_copy(k).start()
        for k in range(BLK):
            in_copy(k).wait()
            out_copy(k).start()
        for k in range(BLK):
            out_copy(k).wait()


def settle_kernel(order, returned, out):
    return pl.pallas_call(
        settle_body,
        out_shape=jax.ShapeDtypeStruct(out.shape, out.dtype),
        in_specs=[SMEM, HBM, HBM],
        out_specs=HBM,
        scratch_shapes=[
            pltpu.VMEM((BLK, SEQ, D), jnp.bfloat16),
            pltpu.SemaphoreType.DMA((BLK,)),
            pltpu.SemaphoreType.DMA((BLK,)),
        ],
        input_output_aliases={2: 0},
        compiler_params=pltpu.CompilerParams(vmem_limit_bytes=VMEM_LIMIT),
        name="settle",
    )(order, returned, out)


def blank(like):
    return pl.pallas_call(
        lambda ref, out: None,
        out_shape=jax.ShapeDtypeStruct(like.shape, like.dtype),
        in_specs=[HBM],
        out_specs=HBM,
        name="blank",
    )(like)


def exchange(chosen, values):
    return lax.cond(
        chosen,
        lambda x: lax.all_to_all(x, "dp", split_axis=0, concat_axis=0, tiled=True),
        blank,
        values,
    )


def local(
    patches, rows, cols, keep, images, destination, row_table, col_table, w_qkv, w_out, w_up, w_down
):
    side = lax.axis_index("fsdp")
    swap = [(0, 1), (1, 0)]
    pairs = []
    for w in (w_qkv, w_out, w_up, w_down):
        pairs.append((w, lax.ppermute(w, "fsdp", swap)))
    table = jnp.transpose(destination, (0, 2, 1))
    sent, order = embed_slots(
        table, table, rows, cols, keep, images, row_table, col_table, patches
    )
    arrived = exchange(side == 0, sent)
    attended = attend_kernel(order, arrived, sent, *pairs[0])
    out, results = mlp_kernel(
        order, table, attended, arrived, sent, *pairs[1], *pairs[2], *pairs[3]
    )
    returned = exchange(side == 1, results)
    return settle_kernel(order, returned, out)


def solution(mesh):
    whole = P(("dp", "fsdp"), None, None)
    flat = P(("dp", "fsdp"), None)
    half = P("fsdp", None)
    in_specs = (
        whole, flat, flat, flat, flat, P("fsdp", None, None), P(), P(), half, half, half, half,
    )
    return jax.shard_map(local, mesh=mesh, in_specs=in_specs, out_specs=whole, check_vma=False)
```

time: 121 us -> 115 us (0.950)
  Pallas kernels: 64.3 us -> 57.3 us
  waiting for transfers between devices: 7.69 us -> 11.7 us
  local copies, waits for them, and re-layouts: 3.74 us -> 1.36 us
  other arithmetic: 1.45 us -> 0 us
    pallas_call x1, Pallas kernels: 35.9 us -> 31.6 us  [mlp_kernel(): pl.pallas_call(mlp_body, out_shape=(jax.ShapeDtypeStruct((BLK, SEQ, D), b...]
    ppermute x4, waiting for transfers between devices: 7.69 us -> 11.7 us  [local(): pairs.append((w, lax.ppermute(w, 'fsdp', swap)))]
    unnamed x5 -> x6, local copies, waits for them, and re-layouts: 3.74 us -> 1.36 us
    pallas_call x1, Pallas kernels: 19.2 us -> 16.9 us  [attend_kernel(): pl.pallas_call(attend_body, out_shape=jax.ShapeDtypeStruct((ROWS, D), bf)...]
  transfers between devices with their start and end apart: 4 -> 4, of which waited for: 1 -> 1; matrix products, arithmetic and copies ran while one was open for 2% -> 0% of each run, Pallas kernels for 21% -> 19%
where the time goes in v2:
time: 115 us; the launch traced here: 114 us
  Pallas kernels  57.3 us (50%)
  blocking collectives  41.6 us (36%)
  waiting for transfers between devices  11.7 us (10%)
  starting transfers between devices  1.89 us (2%)
  local copies, waits for them, and re-layouts  1.36 us (1%)
    all_to_all x1, blocking collectives, exchange(): lax.all_to_all(x, 'dp', split_axis=0, concat_axis=0, tiled=True)  41.6 us
    pallas_call x1, Pallas kernels, mlp_kernel(): pl.pallas_call(mlp_body, out_shape=(jax.ShapeDtypeStruct((BLK, SEQ, D), b...  31.6 us
    pallas_call x1, Pallas kernels, attend_kernel(): pl.pallas_call(attend_body, out_shape=jax.ShapeDtypeStruct((ROWS, D), bf)...  16.9 us
    ppermute x4, waiting for transfers between devices, local(): pairs.append((w, lax.ppermute(w, 'fsdp', swap)))  11.7 us
    pallas_call x1, Pallas kernels, embed_slots(): pl.pallas_call(embed_body, out_shape=(jax.ShapeDtypeStruct((PEERS, SLOT,...  5.17 us
    pallas_call x1, Pallas kernels, settle_kernel(): pl.pallas_call(settle_body, out_shape=jax.ShapeDtypeStruct(out.shape, out...  3.71 us
  transfers between devices with their start and end apart: 4, of which 1 were waited for; matrix products, arithmetic and copies ran while one was open for 0% of the time, Pallas kernels for 19%

profile of v2, /device:TPU:1, one launch (start us, length us, event | category | flops | bytes accessed | tf_op | source)
XLA Modules:
  0.0 114.3 jit_solution(289056576505683158)
XLA Ops:
  0.0 1.4 %collective-permute-start.2 = (bf16[512,4096]{1,0:T(8,128)(2,1)}, bf16[512,4096]{1,0:T(8,128)(2,1)}, u32[]{:S(2)}, u32[]{:S(2)}) collective-permute-start(bf16[512,4096]{1,0:T(8,128)(2,1)} %u0.1), channel_id=1, source_target_pairs={{0,1},{1,0},{2,3},{3,2},{4,5},{5,4},{6,7},{7,6},{8,9},{9,8},{10,11... | collective-permute-start | bytes 12582920 | tf_op jit(solution)/shard_map/ppermute | solution.py:446
  1.4 0.0 collective-permute-start.3
  1.4 0.5 collective-permute-start
  1.9 0.0 collective-permute-start.1
  1.9 5.2 %embed.1 = (bf16[64,264,128]{2,1,0:T(8,128)(2,1)}, s32[32,128]{1,0:T(8,128)}) custom-call(s32[1,32,64]{2,1,0:T(8,128)} %bitcast.1, s32[1,32,64]{2,1,0:T(8,128)} %bitcast.2, s32[32,32]{1,0:T(8,128)} %rows.1, s32[32,32]{1,0:T(8,128)} %cols.1, s32[32,32]{1,0:T(8,128)} %keep.1, s32[32,32]{1,0:T(8,128)} %images.1, bf16[64,1024]{1,0:T(8,128)(2,1)} %row_table.1, ...), custom_call_target="tpu_custom_call" | custom-call | tf_op jit(solution)/shard_map/embed/pallas_call | solution.py:103
  7.1 0.0 copy-start
  7.1 0.0 copy-start.1
  7.1 0.2 conditional.2
  7.3 11.7 %collective-permute-done.other = bf16[512,3072]{1,0:T(8,128)(2,1)} collective-permute-done((bf16[512,3072]{1,0:T(8,128)(2,1)}, bf16[512,3072]{1,0:T(8,128)(2,1)}, u32[]{:S(2)}, u32[]{:S(2)}) %collective-permute-start) | collective-permute-done | bytes 3145760 | tf_op jit(solution)/shard_map/ppermute | solution.py:446
  19.0 0.0 copy-done
  19.0 0.0 copy-done.1
  19.0 16.9 %attend.1.attended = bf16[1024,1024]{1,0:T(8,128)(2,1)S(1)} custom-call(s32[32,128]{1,0:T(8,128)S(1)} %copy-done, bf16[64,264,128]{2,1,0:T(8,128)(2,1)} %get-tuple-element.23.arrived, bf16[64,264,128]{2,1,0:T(8,128)(2,1)} %get-tuple-element.20.sent, bf16[512,3072]{1,0:T(8,128)(2,1)S(1)} %copy-done.1, bf16[512,3072]{1,0:T(8,128)(2,1)} %collective-permute-done.other), custom_call_target="tpu_custom_call" | custom-call | flops 7000000000 | bytes 12000000 | tf_op jit(solution)/shard_map/attend/pallas_call | solution.py:256
  35.9 0.0 copy-start.2
  35.9 1.4 %copy-done.2 = bf16[1024,1024]{1,0:T(8,128)(2,1)} copy-done((bf16[1024,1024]{1,0:T(8,128)(2,1)}, bf16[1024,1024]{1,0:T(8,128)(2,1)S(1)}, u32[]{:S(2)}) %copy-start.2) | copy-done | bytes 2097176
  37.2 0.0 collective-permute-done.1.o1
  37.2 0.0 collective-permute-done.2.u1
  37.2 0.0 collective-permute-done.3.d1
  37.3 31.6 %mlp.1 = (bf16[32,32,1024]{2,1,0:T(8,128)(2,1)}, bf16[64,32,1024]{2,1,0:T(8,128)(2,1)}) custom-call(s32[32,128]{1,0:T(8,128)} %get-tuple-element.19.order, s32[1,32,64]{2,1,0:T(8,128)} %bitcast.3, bf16[1024,1024]{1,0:T(8,128)(2,1)} %copy-done.2, bf16[64,264,128]{2,1,0:T(8,128)(2,1)} %get-tuple-element.23.arrived, ...), custom_call_target="tpu_custom_call" | custom-call | flops 20000000000 | bytes 25000000 | tf_op jit(solution)/shard_map/mlp/pallas_call | solution.py:354
  68.8 41.6 %conditional.3 = (bf16[64,32,1024]{2,1,0:T(8,128)(2,1)}) conditional(s32[]{:T(128)} %convert_element_type.6, bf16[64,32,1024]{2,1,0:T(8,128)(2,1)} %get-tuple-element.21, bf16[64,32,1024]{2,1,0:T(8,128)(2,1)} %get-tuple-element.21), branch_computations={%region_2.0_spmd, %region_3.0_spmd} | conditional | bytes 8388616 | solution.py:431
  68.8 41.6 %all_to_all.9 = bf16[64,32,1024]{2,1,0:T(8,128)(2,1)} all-to-all(bf16[64,32,1024]{2,1,0:T(8,128)(2,1)} %param.3), channel_id=1, replica_groups=mesh['dp'=64,'fsdp'=2] {'dp'}, dimensions={0} | all-to-all | bytes 8388608 | tf_op jit(solution)/shard_map/cond/branch_1_fun/all_to_all | solution.py:433
  110.4 3.7 %settle.1 = bf16[32,32,1024]{2,1,0:T(8,128)(2,1)} custom-call(s32[32,128]{1,0:T(8,128)} %get-tuple-element.19.order, bf16[64,32,1024]{2,1,0:T(8,128)(2,1)} %get-tuple-element.24.returned, bf16[32,32,1024]{2,1,0:T(8,128)(2,1)} %get-tuple-element.22.out_in), custom_call_target="tpu_custom_call", output_to_operand_aliasing={{}: (2, {})} | custom-call | tf_op jit(solution)/shard_map/settle/pallas_call | solution.py:404
  (1 shorter events, 0.0 us)
Async XLA Ops:
  0.0 37.2 %collective-permute-start.2 = (bf16[512,4096]{1,0:T(8,128)(2,1)}, bf16[512,4096]{1,0:T(8,128)(2,1)}, u32[]{:S(2)}, u32[]{:S(2)}) collective-permute-start(bf16[512,4096]{1,0:T(8,128)(2,1)} %u0.1), channel_id=1, source_target_pairs={{0,1},{1,0},{2,3},{3,2},{4,5},{5,4},{6,7},{7,6},{8,9},{9,8},{10,11... | collective-permute-start | bytes 12582920 | tf_op jit(solution)/shard_map/ppermute | solution.py:446
  1.4 35.9 %collective-permute-start.3 = (bf16[2048,1024]{1,0:T(8,128)(2,1)}, bf16[2048,1024]{1,0:T(8,128)(2,1)}, u32[]{:S(2)}, u32[]{:S(2)}) collective-permute-start(bf16[2048,1024]{1,0:T(8,128)(2,1)} %d0.1), channel_id=1, source_target_pairs={{0,1},{1,0},{2,3},{3,2},{4,5},{5,4},{6,7},{7,6},{8,9},{9,8},{10,11... | collective-permute-start | bytes 12582920 | tf_op jit(solution)/shard_map/ppermute | solution.py:446
  1.4 17.6 %collective-permute-start = (bf16[512,3072]{1,0:T(8,128)(2,1)}, bf16[512,3072]{1,0:T(8,128)(2,1)}, u32[]{:S(2)}, u32[]{:S(2)}) collective-permute-start(bf16[512,3072]{1,0:T(8,128)(2,1)} %own.1), channel_id=1, source_target_pairs={{0,1},{1,0},{2,3},{3,2},{4,5},{5,4},{6,7},{7,6},{8,9},{9,8},{10,11... | collective-permute-start | bytes 9437192 | tf_op jit(solution)/shard_map/ppermute | solution.py:446
  1.9 35.3 %collective-permute-start.1 = (bf16[512,1024]{1,0:T(8,128)(2,1)}, bf16[512,1024]{1,0:T(8,128)(2,1)}, u32[]{:S(2)}, u32[]{:S(2)}) collective-permute-start(bf16[512,1024]{1,0:T(8,128)(2,1)} %o0.1), channel_id=1, source_target_pairs={{0,1},{1,0},{2,3},{3,2},{4,5},{5,4},{6,7},{7,6},{8,9},{9,8},{10,11... | collective-permute-start | bytes 3145736 | tf_op jit(solution)/shard_map/ppermute | solution.py:446
  7.1 11.9 %copy-start = (s32[32,128]{1,0:T(8,128)S(1)}, s32[32,128]{1,0:T(8,128)}, u32[]{:S(2)}) copy-start(s32[32,128]{1,0:T(8,128)} %get-tuple-element.19.order) | copy-start | bytes 49156
  7.1 11.9 %copy-start.1 = (bf16[512,3072]{1,0:T(8,128)(2,1)S(1)}, bf16[512,3072]{1,0:T(8,128)(2,1)}, u32[]{:S(2)}) copy-start(bf16[512,3072]{1,0:T(8,128)(2,1)} %own.1) | copy-start | bytes 9437188
  35.9 1.4 %copy-start.2 = (bf16[1024,1024]{1,0:T(8,128)(2,1)}, bf16[1024,1024]{1,0:T(8,128)(2,1)S(1)}, u32[]{:S(2)}) copy-start(bf16[1024,1024]{1,0:T(8,128)(2,1)S(1)} %attend.1.attended) | copy-start | bytes 6291460

commit v3 on v2

--- a/solution.py
+++ b/solution.py
@@ -23,8 +23,14 @@
 DOWN = 256
 MASKED = -1e30
 VMEM_LIMIT = 60 * 1024 * 1024
-ATTEND_LIMIT = 36 * 1024 * 1024
+EMBED_LIMIT = 60 * 1024 * 1024
+ATTEND_LIMIT = 24 * 1024 * 1024
+MLP_LIMIT = 34 * 1024 * 1024
 WIDE = 512
+RB = 256
+RS = RB // SEQ
+QB = 512
+QS = QB // SEQ
 ANY = pl.BlockSpec(memory_space=pl.ANY)
 HBM = pl.BlockSpec(memory_space=pltpu.HBM)
 SMEM = pl.BlockSpec(memory_space=pltpu.SMEM)
@@ -44,8 +50,9 @@
 
 
 def embed_body(
-    table, wide_table, rows, cols, keep, images, row_table, col_table, patches, out, order,
-    buf, raw, tables, marks, spots, in_sem, sem,
+    table, wide_in, rows_in, cols_in, keep_in, images_in, row_table, col_table, patches,
+    out, order,
+    buf, raw, tables, marks, spots, wide_table, rows, cols, keep, images, in_sem, small_sem, sem,
 ):
     me, side = lax.axis_index("dp"), lax.axis_index("fsdp")
 
@@ -57,10 +64,18 @@
         slot = jnp.where(side == 0, table[0, k, me], k)
         return pltpu.make_async_copy(buf.at[k], out.at[slot], sem.at[k])
 
+    small = [
+        (keep_in, keep), (images_in, images), (rows_in, rows), (cols_in, cols),
+        (row_table, tables.at[:GRID, :]), (col_table, tables.at[GRID:, :]), (wide_in, wide_table),
+    ]
+    small = [
+        pltpu.make_async_copy(source, target, small_sem.at[i])
+        for i, (source, target) in enumerate(small)
+    ]
+    run(small, "start")
     for g in range(BLK // GROUP // 2):
         in_copy(g).start()
-    tables[:GRID, :] = row_table[...]
-    tables[GRID:, :] = col_table[...]
+    run(small, "wait")
     label = (keep[...] * (images[...] + 1)).astype(jnp.float32)
     marks[...] = jnp.concatenate([label] * GROUP, axis=1)
     for i, ref in enumerate((rows, cols)):
@@ -106,7 +121,7 @@
             jax.ShapeDtypeStruct((PEERS, SLOT, 128), jnp.bfloat16),
             jax.ShapeDtypeStruct((BLK, 128), jnp.int32),
         ),
-        in_specs=[SMEM] + [VMEM] * 7 + [HBM],
+        in_specs=[SMEM] + [ANY] * 8,
         out_specs=(HBM, VMEM),
         scratch_shapes=[
             pltpu.VMEM((BLK, SLOT, 128), jnp.bfloat16),
@@ -114,10 +129,16 @@
             pltpu.VMEM((2 * GRID, D), jnp.bfloat16),
             pltpu.VMEM((BLK, 128), jnp.float32),
             pltpu.VMEM((2, BLK // GROUP, 128), jnp.int32),
+            pltpu.VMEM((1, BLK, PEERS), jnp.int32),
+            pltpu.VMEM((BLK, SEQ), jnp.int32),
+            pltpu.VMEM((BLK, SEQ), jnp.int32),
+            pltpu.VMEM((BLK, SEQ), jnp.int32),
+            pltpu.VMEM((BLK, SEQ), jnp.int32),
             pltpu.SemaphoreType.DMA((BLK // GROUP // 2,)),
+            pltpu.SemaphoreType.DMA((7,)),
             pltpu.SemaphoreType.DMA((BLK,)),
         ],
-        compiler_params=pltpu.CompilerParams(vmem_limit_bytes=VMEM_LIMIT),
+        compiler_params=pltpu.CompilerParams(vmem_limit_bytes=EMBED_LIMIT),
         name="embed",
     )(*operands)
 
@@ -167,8 +188,8 @@
 
 
 def attend_body(
-    order, arrived, sent, own, other, out,
-    xs, w_qkv, normed, qkv, mixed, in_sem, w_sem, out_sem,
+    order, arrived, sent, own, other, out, kept,
+    xs, w_qkv, normed, qkv, mixed, in_sem, w_sem, out_sem, keep_sem,
 ):
     side = lax.axis_index("fsdp")
     copies = weight_copies(side, own, other, w_qkv, w_sem.at[0])
@@ -177,29 +198,31 @@
         part = pl.ds(g * 128, 128)
         return pltpu.make_async_copy(mixed.at[part, :], out.at[part, :], out_sem.at[g])
 
-    load_sequences(side, order, arrived, sent, xs, in_sem, 0, 8)
+    load_sequences(side, order, arrived, sent, xs, in_sem, 0, QS)
     run(copies, "start")
-    load_sequences(side, order, arrived, sent, xs, in_sem, 8, BLK)
+    load_sequences(side, order, arrived, sent, xs, in_sem, QS, BLK)
 
     def smooth(m, slot):
-        for j in range(8):
-            x = sequence(xs, m * 8 + j).astype(jnp.float32)
+        for j in range(QS):
+            x = sequence(xs, m * QS + j).astype(jnp.float32)
             normed[slot, j * SEQ:(j + 1) * SEQ, :] = norm(x).astype(jnp.bfloat16)
 
     def project(m, slot):
-        base = m * 256 if isinstance(m, int) else pl.multiple_of(m * 256, 256)
+        base = m * QB if isinstance(m, int) else pl.multiple_of(m * QB, QB)
         for n in range(3 * D // WIDE):
             part = jnp.dot(
                 normed[slot], w_qkv[:, n * WIDE:(n + 1) * WIDE],
                 preferred_element_type=jnp.float32,
             )
-            qkv[pl.ds(base, 256), n * WIDE:(n + 1) * WIDE] = part.astype(jnp.bfloat16)
-
-    for j in range(8):
+            qkv[pl.ds(base, QB), n * WIDE:(n + 1) * WIDE] = part.astype(jnp.bfloat16)
+
+    for j in range(QS):
         await_sequence(sent, xs, in_sem, j)
     smooth(0, 0)
-    for j in range(8, BLK):
+    for j in range(QS, BLK):
         await_sequence(sent, xs, in_sem, j)
+    keeping = pltpu.make_async_copy(xs, kept, keep_sem)
+    keeping.start()
     run(copies, "wait")
 
     def block(m, carry):
@@ -208,8 +231,8 @@
         smooth(m + 1, 1 - slot)
         return carry
 
-    lax.fori_loop(0, 3, block, 0)
-    project(3, 1)
+    lax.fori_loop(0, ROWS // QB - 1, block, 0)
+    project(ROWS // QB - 1, 1)
     lane = lax.broadcasted_iota(jnp.int32, (128, 128), 1)
     line = lax.broadcasted_iota(jnp.int32, (128, 128), 0)
     low = lane < HEAD_DIM
@@ -249,24 +272,29 @@
     lax.fori_loop(0, BLK // GROUP, attend, 0)
     for g in range(BLK // GROUP):
         out_copy(g).wait()
+    keeping.wait()
 
 
 def attend_kernel(order, arrived, sent, own, other):
     bf = jnp.bfloat16
     return pl.pallas_call(
         attend_body,
-        out_shape=jax.ShapeDtypeStruct((ROWS, D), bf),
+        out_shape=(
+            jax.ShapeDtypeStruct((ROWS, D), bf),
+            jax.ShapeDtypeStruct((BLK, SLOT, 128), bf),
+        ),
         in_specs=[SMEM, HBM, HBM, ANY, ANY],
-        out_specs=HBM,
+        out_specs=(ANY, ANY),
         scratch_shapes=[
             pltpu.VMEM((BLK, SLOT, 128), bf),
             pltpu.VMEM((D, 3 * D), bf),
-            pltpu.VMEM((2, 256, D), bf),
+            pltpu.VMEM((2, QB, D), bf),
             pltpu.VMEM((ROWS, 3 * D), bf),
             pltpu.VMEM((ROWS, D), bf),
             pltpu.SemaphoreType.DMA((BLK,)),
             pltpu.SemaphoreType.DMA((1, 2)),
             pltpu.SemaphoreType.DMA((BLK // GROUP,)),
+            pltpu.SemaphoreType.DMA,
         ],
         cost_estimate=pl.CostEstimate(
             flops=7_000_000_000, bytes_accessed=12_000_000, transcendentals=2_000_000
@@ -277,7 +305,7 @@
 
 
 def mlp_body(
-    order, table, attended, arrived, sent, o0, o1, u0, u1, d0, d1, out, results,
+    table, attended, kept, o0, o1, u0, u1, d0, d1, out, results,
     xs, w_out, w_up, w_down, normed, second, mid, act, outb, in_sem, w_sem, out_sem, mix_sem,
 ):
     me, side = lax.axis_index("dp"), lax.axis_index("fsdp")
@@ -286,30 +314,33 @@
     downs = weight_copies(side, d0, d1, w_down, w_sem.at[2])
 
     def mix_copy(m):
-        part = pl.ds(m * 256, 256)
+        part = pl.ds(m * RB, RB)
         return pltpu.make_async_copy(attended.at[part, :], normed.at[part, :], mix_sem.at[m])
+
+    def part_copy(m):
+        part = pl.ds(m * RS, RS)
+        return pltpu.make_async_copy(kept.at[part], xs.at[part], in_sem.at[m])
 
     mix_copy(0).start()
     run(proj, "start")
-    load_sequences(side, order, arrived, sent, xs, in_sem, 0, 8)
+    part_copy(0).start()
     run(ups + downs, "start")
-    load_sequences(side, order, arrived, sent, xs, in_sem, 8, BLK)
-    for m in range(1, 4):
+    for m in range(1, ROWS // RB):
+        part_copy(m).start()
         mix_copy(m).start()
 
     def block(m, first):
-        base = m * 256 if first else pl.multiple_of(m * 256, 256)
+        base = m * RB if first else pl.multiple_of(m * RB, RB)
         mix_copy(m).wait()
         if first:
             run(proj, "wait")
-        for j in range(8):
-            await_sequence(sent, xs, in_sem, m * 8 + j)
-        columns = jnp.concatenate([marks_of(xs, m * 2 + g)[1] for g in range(2)], axis=0)
+        part_copy(m).wait()
+        columns = jnp.concatenate([marks_of(xs, m * (RB // 128) + g)[1] for g in range(RB // 128)], axis=0)
         part = jnp.dot(
-            normed[pl.ds(base, 256), :], w_out[...], preferred_element_type=jnp.float32
+            normed[pl.ds(base, RB), :], w_out[...], preferred_element_type=jnp.float32
         )
-        for j in range(8):
-            k = m * 8 + j
+        for j in range(RS):
+            k = m * RS + j
             total = sequence(xs, k).astype(jnp.float32) + part[j * SEQ:(j + 1) * SEQ, :]
             mid[j * SEQ:(j + 1) * SEQ, :] = total
             second[j * SEQ:(j + 1) * SEQ, :] = norm(total).astype(jnp.bfloat16)
@@ -328,10 +359,10 @@
             )
             total = mid[:, n * DOWN:(n + 1) * DOWN] + lower
             total = jnp.where(columns > 0.0, total, 0.0).astype(jnp.bfloat16)
-            for j in range(8):
-                outb[m * 8 + j, :, n * DOWN:(n + 1) * DOWN] = total[j * SEQ:(j + 1) * SEQ, :]
-        for j in range(8):
-            k = m * 8 + j
+            for j in range(RS):
+                outb[m * RS + j, :, n * DOWN:(n + 1) * DOWN] = total[j * SEQ:(j + 1) * SEQ, :]
+        for j in range(RS):
+            k = m * RS + j
 
             @pl.when(side == 0)
             def _():
@@ -344,7 +375,7 @@
                 ).start()
 
     block(0, True)
-    lax.fori_loop(1, 4, lambda m, carry: (block(m, False), carry)[1], 0)
+    lax.fori_loop(1, ROWS // RB, lambda m, carry: (block(m, False), carry)[1], 0)
     for k in range(BLK):
         pltpu.make_async_copy(outb.at[k], out.at[k], out_sem.at[k]).wait()
 
@@ -357,7 +388,7 @@
             jax.ShapeDtypeStruct((BLK, SEQ, D), bf),
             jax.ShapeDtypeStruct((PEERS, SEQ, D), bf),
         ),
-        in_specs=[SMEM, SMEM, ANY] + [HBM] * 8,
+        in_specs=[SMEM] + [ANY] * 8,
         out_specs=(HBM, HBM),
         scratch_shapes=[
             pltpu.VMEM((BLK, SLOT, 128), bf),
@@ -365,19 +396,19 @@
             pltpu.VMEM((D, MLP), bf),
             pltpu.VMEM((MLP, D), bf),
             pltpu.VMEM((ROWS, D), bf),
-            pltpu.VMEM((256, D), bf),
-            pltpu.VMEM((256, D), f32),
-            pltpu.VMEM((256, MLP), bf),
+            pltpu.VMEM((RB, D), bf),
+            pltpu.VMEM((RB, D), f32),
+            pltpu.VMEM((RB, MLP), bf),
             pltpu.VMEM((BLK, SEQ, D), bf),
-            pltpu.SemaphoreType.DMA((BLK,)),
+            pltpu.SemaphoreType.DMA((ROWS // RB,)),
             pltpu.SemaphoreType.DMA((3, 2)),
             pltpu.SemaphoreType.DMA((BLK,)),
-            pltpu.SemaphoreType.DMA((4,)),
+            pltpu.SemaphoreType.DMA((ROWS // RB,)),
         ],
         cost_estimate=pl.CostEstimate(
             flops=20_000_000_000, bytes_accessed=25_000_000, transcendentals=4_000_000
         ),
-        compiler_params=pltpu.CompilerParams(vmem_limit_bytes=VMEM_LIMIT),
+        compiler_params=pltpu.CompilerParams(vmem_limit_bytes=MLP_LIMIT),
         name="mlp",
     )(*operands)
 
@@ -449,10 +480,8 @@
         table, table, rows, cols, keep, images, row_table, col_table, patches
     )
     arrived = exchange(side == 0, sent)
-    attended = attend_kernel(order, arrived, sent, *pairs[0])
-    out, results = mlp_kernel(
-        order, table, attended, arrived, sent, *pairs[1], *pairs[2], *pairs[3]
-    )
+    attended, kept = attend_kernel(order, arrived, sent, *pairs[0])
+    out, results = mlp_kernel(table, attended, kept, *pairs[1], *pairs[2], *pairs[3])
     returned = exchange(side == 1, results)
     return settle_kernel(order, returned, out)
 

time: 115 us -> 110 us (0.957)
  Pallas kernels: 57.3 us -> 54.7 us
  local copies, waits for them, and re-layouts: 1.36 us -> 0.03 us
    pallas_call x1, Pallas kernels: 31.6 us -> 28.6 us  [mlp_kernel(): pl.pallas_call(mlp_body, out_shape=(jax.ShapeDtypeStruct((BLK, SEQ, D), b...]
    unnamed x6 -> x12, local copies, waits for them, and re-layouts: 1.36 us -> 0.03 us
  transfers between devices with their start and end apart: 4 -> 4, of which waited for: 1 -> 1; matrix products, arithmetic and copies ran while one was open for 0% -> 0% of each run, Pallas kernels for 19% -> 20%
where the time goes in v3:
time: 110 us
  Pallas kernels  54.7 us (50%)
  blocking collectives  41.6 us (38%)
  waiting for transfers between devices  11.3 us (10%)
  starting transfers between devices  1.89 us (2%)
    all_to_all x1, blocking collectives, exchange(): lax.all_to_all(x, 'dp', split_axis=0, concat_axis=0, tiled=True)  41.6 us
    pallas_call x1, Pallas kernels, mlp_kernel(): pl.pallas_call(mlp_body, out_shape=(jax.ShapeDtypeStruct((BLK, SEQ, D), b...  28.6 us
    pallas_call x1, Pallas kernels, attend_kernel(): pl.pallas_call(attend_body, out_shape=(jax.ShapeDtypeStruct((ROWS, D), bf...  16.8 us
    ppermute x4, waiting for transfers between devices, local(): pairs.append((w, lax.ppermute(w, 'fsdp', swap)))  11.3 us
    pallas_call x1, Pallas kernels, embed_slots(): pl.pallas_call(embed_body, out_shape=(jax.ShapeDtypeStruct((PEERS, SLOT,...  5.54 us
    pallas_call x1, Pallas kernels, settle_kernel(): pl.pallas_call(settle_body, out_shape=jax.ShapeDtypeStruct(out.shape, out...  3.71 us
  transfers between devices with their start and end apart: 4, of which 1 were waited for; matrix products, arithmetic and copies ran while one was open for 0% of the time, Pallas kernels for 20%

profile of v3, /device:TPU:1, one launch (start us, length us, event | category | flops | bytes accessed | tf_op | source)
XLA Modules:
  0.0 110.1 jit_solution(7945855950175733306)
XLA Ops:
  0.0 1.4 %collective-permute-start.2 = (bf16[512,4096]{1,0:T(8,128)(2,1)}, bf16[512,4096]{1,0:T(8,128)(2,1)}, u32[]{:S(2)}, u32[]{:S(2)}) collective-permute-start(bf16[512,4096]{1,0:T(8,128)(2,1)} %u0.1), channel_id=1, source_target_pairs={{0,1},{1,0},{2,3},{3,2},{4,5},{5,4},{6,7},{7,6},{8,9},{9,8},{10,11... | collective-permute-start | bytes 12582920 | tf_op jit(solution)/shard_map/ppermute | solution.py:477
  1.4 0.0 collective-permute-start.3
  1.4 0.5 collective-permute-start
  1.9 0.0 collective-permute-start.1
  1.9 5.5 %embed.1 = (bf16[64,264,128]{2,1,0:T(8,128)(2,1)}, s32[32,128]{1,0:T(8,128)}) custom-call(s32[1,32,64]{2,1,0:T(8,128)} %bitcast.1, s32[1,32,64]{2,1,0:T(8,128)} %bitcast.2, s32[32,32]{1,0:T(8,128)} %rows_in.1, s32[32,32]{1,0:T(8,128)} %cols_in.1, s32[32,32]{1,0:T(8,128)} %keep_in.1, s32[32,32]{1,0:T(8,128)} %images_in.1, bf16[64,1024]{1,0:T(8,128)(2,1)} %row_table.1, ...), custom_call_target="tpu_custom_call" | custom-call | tf_op jit(solution)/shard_map/embed/pallas_call | solution.py:118
  7.4 0.0 copy-start.1
  7.5 0.0 copy-start.4
  7.5 0.2 conditional.2
  7.7 11.3 %collective-permute-done.other = bf16[512,3072]{1,0:T(8,128)(2,1)} collective-permute-done((bf16[512,3072]{1,0:T(8,128)(2,1)}, bf16[512,3072]{1,0:T(8,128)(2,1)}, u32[]{:S(2)}, u32[]{:S(2)}) %collective-permute-start) | collective-permute-done | bytes 3145760 | tf_op jit(solution)/shard_map/ppermute | solution.py:477
  19.0 0.0 copy-done.1
  19.0 0.0 copy-done.4
  19.0 0.0 copy-start
  19.0 0.0 copy-start.2
  19.0 0.0 copy-start.3
  19.0 0.0 copy-start.5
  19.0 16.8 %attend.1 = (bf16[1024,1024]{1,0:T(8,128)(2,1)S(1)}, bf16[32,264,128]{2,1,0:T(8,128)(2,1)S(1)}) custom-call(s32[32,128]{1,0:T(8,128)S(1)} %copy-done.1, bf16[64,264,128]{2,1,0:T(8,128)(2,1)} %get-tuple-element.27.arrived, bf16[64,264,128]{2,1,0:T(8,128)(2,1)} %get-tuple-element.22.sent, bf16[512,3072]{1,0:T(8,128)(2,1)S(1)} %copy-done.4, ...), custom_call_target="tpu_custom_call" | custom-call | flops 7000000000 | bytes 12000000 | tf_op jit(solution)/shard_map/attend/pallas_call | solution.py:280
  35.9 0.0 collective-permute-done.1.o1
  35.9 0.0 collective-permute-done.2.u1
  35.9 0.0 collective-permute-done.3.d1
  35.9 0.0 copy-done
  35.9 0.0 copy-done.2
  35.9 0.0 copy-done.3
  35.9 0.0 copy-done.5
  35.9 28.6 %mlp.1 = (bf16[32,32,1024]{2,1,0:T(8,128)(2,1)}, bf16[64,32,1024]{2,1,0:T(8,128)(2,1)}) custom-call(s32[1,32,64]{2,1,0:T(8,128)S(1)} %bitcast.3, bf16[1024,1024]{1,0:T(8,128)(2,1)S(1)} %get-tuple-element.23.attended, bf16[32,264,128]{2,1,0:T(8,128)(2,1)S(1)} %get-tuple-element.24.kept, bf16[512,1024]{1,0:T(8,128)(2,1)S(1)} %copy-done.5, ...), custom_call_target="tpu_custom_call" | custom-call | flops 20000000000 | bytes 25000000 | tf_op jit(solution)/shard_map/mlp/pallas_call | solution.py:385
  64.6 41.6 %conditional.3 = (bf16[64,32,1024]{2,1,0:T(8,128)(2,1)}) conditional(s32[]{:T(128)} %convert_element_type.6, bf16[64,32,1024]{2,1,0:T(8,128)(2,1)} %get-tuple-element.25, bf16[64,32,1024]{2,1,0:T(8,128)(2,1)} %get-tuple-element.25), branch_computations={%region_2.0_spmd, %region_3.0_spmd} | conditional | bytes 8388616 | solution.py:462
  64.6 41.6 %all_to_all.9 = bf16[64,32,1024]{2,1,0:T(8,128)(2,1)} all-to-all(bf16[64,32,1024]{2,1,0:T(8,128)(2,1)} %param.3), channel_id=1, replica_groups=mesh['dp'=64,'fsdp'=2] {'dp'}, dimensions={0} | all-to-all | bytes 8388608 | tf_op jit(solution)/shard_map/cond/branch_1_fun/all_to_all | solution.py:464
  106.2 3.7 %settle.1 = bf16[32,32,1024]{2,1,0:T(8,128)(2,1)} custom-call(s32[32,128]{1,0:T(8,128)} %get-tuple-element.21.order, bf16[64,32,1024]{2,1,0:T(8,128)(2,1)} %get-tuple-element.28.returned, bf16[32,32,1024]{2,1,0:T(8,128)(2,1)} %get-tuple-element.26.out_in), custom_call_target="tpu_custom_call", output_to_operand_aliasing={{}: (2, {})} | custom-call | tf_op jit(solution)/shard_map/settle/pallas_call | solution.py:435
  (1 shorter events, 0.0 us)
Async XLA Ops:
  0.0 35.9 %collective-permute-start.2 = (bf16[512,4096]{1,0:T(8,128)(2,1)}, bf16[512,4096]{1,0:T(8,128)(2,1)}, u32[]{:S(2)}, u32[]{:S(2)}) collective-permute-start(bf16[512,4096]{1,0:T(8,128)(2,1)} %u0.1), channel_id=1, source_target_pairs={{0,1},{1,0},{2,3},{3,2},{4,5},{5,4},{6,7},{7,6},{8,9},{9,8},{10,11... | collective-permute-start | bytes 12582920 | tf_op jit(solution)/shard_map/ppermute | solution.py:477
  1.4 34.5 %collective-permute-start.3 = (bf16[2048,1024]{1,0:T(8,128)(2,1)}, bf16[2048,1024]{1,0:T(8,128)(2,1)}, u32[]{:S(2)}, u32[]{:S(2)}) collective-permute-start(bf16[2048,1024]{1,0:T(8,128)(2,1)} %d0.1), channel_id=1, source_target_pairs={{0,1},{1,0},{2,3},{3,2},{4,5},{5,4},{6,7},{7,6},{8,9},{9,8},{10,11... | collective-permute-start | bytes 12582920 | tf_op jit(solution)/shard_map/ppermute | solution.py:477
  1.4 17.6 %collective-permute-start = (bf16[512,3072]{1,0:T(8,128)(2,1)}, bf16[512,3072]{1,0:T(8,128)(2,1)}, u32[]{:S(2)}, u32[]{:S(2)}) collective-permute-start(bf16[512,3072]{1,0:T(8,128)(2,1)} %own.1), channel_id=1, source_target_pairs={{0,1},{1,0},{2,3},{3,2},{4,5},{5,4},{6,7},{7,6},{8,9},{9,8},{10,11... | collective-permute-start | bytes 9437192 | tf_op jit(solution)/shard_map/ppermute | solution.py:477
  1.9 34.0 %collective-permute-start.1 = (bf16[512,1024]{1,0:T(8,128)(2,1)}, bf16[512,1024]{1,0:T(8,128)(2,1)}, u32[]{:S(2)}, u32[]{:S(2)}) collective-permute-start(bf16[512,1024]{1,0:T(8,128)(2,1)} %o0.1), channel_id=1, source_target_pairs={{0,1},{1,0},{2,3},{3,2},{4,5},{5,4},{6,7},{7,6},{8,9},{9,8},{10,11... | collective-permute-start | bytes 3145736 | tf_op jit(solution)/shard_map/ppermute | solution.py:477
  7.4 11.6 %copy-start.1 = (s32[32,128]{1,0:T(8,128)S(1)}, s32[32,128]{1,0:T(8,128)}, u32[]{:S(2)}) copy-start(s32[32,128]{1,0:T(8,128)} %get-tuple-element.21.order) | copy-start | bytes 49156
  7.5 11.6 %copy-start.4 = (bf16[512,3072]{1,0:T(8,128)(2,1)S(1)}, bf16[512,3072]{1,0:T(8,128)(2,1)}, u32[]{:S(2)}) copy-start(bf16[512,3072]{1,0:T(8,128)(2,1)} %own.1) | copy-start | bytes 9437188
  19.0 16.9 %copy-start = (s32[1,64,32]{1,2,0:T(8,128)S(1)}, s32[1,64,32]{1,2,0:T(8,128)}, u32[]{:S(2)}) copy-start(s32[1,64,32]{1,2,0:T(8,128)} %param.21) | copy-start | bytes 24580
  19.0 16.9 %copy-start.2 = (bf16[512,4096]{1,0:T(8,128)(2,1)S(1)}, bf16[512,4096]{1,0:T(8,128)(2,1)}, u32[]{:S(2)}) copy-start(bf16[512,4096]{1,0:T(8,128)(2,1)} %u0.1) | copy-start | bytes 12582916
  19.0 16.9 %copy-start.3 = (bf16[2048,1024]{1,0:T(8,128)(2,1)S(1)}, bf16[2048,1024]{1,0:T(8,128)(2,1)}, u32[]{:S(2)}) copy-start(bf16[2048,1024]{1,0:T(8,128)(2,1)} %d0.1) | copy-start | bytes 12582916
  19.0 16.9 %copy-start.5 = (bf16[512,1024]{1,0:T(8,128)(2,1)S(1)}, bf16[512,1024]{1,0:T(8,128)(2,1)}, u32[]{:S(2)}) copy-start(bf16[512,1024]{1,0:T(8,128)(2,1)} %o0.1) | copy-start | bytes 3145732
